TPU v7x, 256 devices: a whole 4x4x8 slice. The times are simulated.
256 devices in a mesh: pp: 2 (over core), ep: 64 (over x, z_lo, y), tp: 2 (over z_hi).
Axes of the slice: x: 4, y: 4, z: 8 (z_hi: 2, z_lo: 4; z = z_hi * 4 + z_lo), core: 2. Of those that a mesh axis runs over, the one named last changes fastest.
Arguments:
- acts: bfloat16 [2, 384, 3072], P(None, 'ep'), may hold values from -6 to 6
- route_ids: int32 [2, 2, 384, 8], P('pp', None, 'ep'), may hold values from 0 to 95, all different within a row; in each aligned block of 6 rows (0 to 5, 6 to 11, ..., all dimensions but the last counted through in order) at most 2 rows name the same one
- norm_gain: bfloat16 [2, 3072], P('pp'), may hold values from 0.5 to 1.5
- router: bfloat16 [2, 3072, 96], P('pp'), may hold values from -0.109375 to 0.109375
- dense_gate: bfloat16 [2, 3072, 6144], P('pp', None, ('ep', 'tp')), may hold values from -0.109375 to 0.109375
- dense_up: bfloat16 [2, 3072, 6144], P('pp', None, ('ep', 'tp')), may hold values from -0.109375 to 0.109375
- dense_down: bfloat16 [2, 6144, 3072], P('pp', ('ep', 'tp')), may hold values from -0.078125 to 0.078125
- expert_gate: bfloat16 [2, 64, 3072, 1024], P('pp', 'ep', None, 'tp'), may hold values from -0.109375 to 0.109375
- expert_up: bfloat16 [2, 64, 3072, 1024], P('pp', 'ep', None, 'tp'), may hold values from -0.109375 to 0.109375
- expert_down: bfloat16 [2, 64, 1024, 3072], P('pp', 'ep', 'tp'), may hold values from -0.1875 to 0.1875
Outputs:
- layer_out: bfloat16 [2, 2, 384, 3072], P('pp', None, 'ep')
Inputs may be any that keep to these rules, and one draw needn't show every extreme that they name: `route_ids`: the 8 ids of a token differ. In each layer and microbatch, among the 6 tokens of one ep index no id is named by more than 2 tokens, a bound that some block reaches.
All inputs are finite; a program needn't handle non-finite values.
Results may differ from a plain program's by a relative error of at most 0.008.
Values may be sent and summed in bfloat16 or wider, within the bound.
A program may use at most 128 MiB of HBM per device.

v0:
```python
import jax
import jax.numpy as jnp
from jax import lax
from jax.sharding import Mesh
from jax.sharding import PartitionSpec as P

EP = ("ep_0", "ep_1", "ep_2")
EP_TP = ("ep_0", "ep_1", "ep_2", "tp")


def sent_to_all(shard, axis):
    copies = jnp.broadcast_to(shard, (lax.axis_size(axis), *shard.shape))
    return lax.all_to_all(copies, axis, split_axis=0, concat_axis=0, tiled=True)


def joined_along(tiles, dim):
    lengths = list(tiles.shape[1:])
    lengths[dim] *= tiles.shape[0]
    return jnp.moveaxis(tiles, 0, dim).reshape(lengths)


def gathered_copies(shard, axis, dim):
    tiles = sent_to_all(shard, axis)
    return joined_along(tiles, dim)


def in_blocks(shard, dim, length):
    before, after = (shard.shape[:dim], shard.shape[dim + 1 :])
    return jnp.moveaxis(shard.reshape(*before, length, -1, *after), dim, 0)


def sum_at_owner(shard, axis, dim):
    length = lax.axis_size(axis)
    tiles = lax.all_to_all(in_blocks(shard, dim, length), axis, 0, 0, tiled=True)
    return jnp.sum(tiles, axis=0)


def sum_in_two_steps(shard, axes, dim):
    far, near = axes
    return sum_at_owner(sum_at_owner(shard, far, dim), near, dim)


def from_behind(block, axis, distance):
    devices = range(lax.axis_size(axis))
    route = [(i - distance, i) for i in devices if i - distance in devices]
    return lax.ppermute(block, axis, route)


def normalize(inputs, gain):
    widened = inputs.astype(jnp.float32)
    spread = jnp.mean(widened * widened, axis=-1, keepdims=True)
    normed = (widened * lax.rsqrt(spread + 1e-06) * gain.astype(jnp.float32)).astype(jnp.bfloat16)
    return (widened, normed)


def gated_block(inputs, w_gate, w_up, w_down):
    gate_part = jnp.dot(inputs, w_gate, preferred_element_type=jnp.float32)
    up_part = jnp.dot(inputs, w_up, preferred_element_type=jnp.float32)
    hidden = (jax.nn.silu(gate_part) * up_part).astype(jnp.bfloat16)
    return jnp.dot(hidden, w_down, preferred_element_type=jnp.float32)


def choice_weights(normed, route_rows, router_w, n_real):
    n_total = router_w.shape[1]
    gates = jax.nn.sigmoid(jnp.dot(normed, router_w, preferred_element_type=jnp.float32))
    picked = (route_rows[:, :, None] == jnp.arange(n_total, dtype=jnp.int32)[None, None, :]).astype(
        jnp.float32
    )
    weights = jnp.sum(picked * gates[:, None, :], axis=-1)
    zero_share = jnp.sum(jnp.where(route_rows >= n_real, weights, jnp.float32(0.0)), axis=-1)
    return (weights, picked, zero_share)


def on_device(
    acts,
    route_ids,
    norm_gain,
    router,
    dense_gate,
    dense_up,
    dense_down,
    expert_gate,
    expert_up,
    expert_down,
):
    n_micro, per_group, width = acts.shape
    top_count = route_ids.shape[-1]
    n_groups = lax.axis_size(EP)
    n_pairs = lax.axis_size("tp")
    section = lax.axis_index("pp")
    group_pos = lax.axis_index(EP)
    pair_pos = lax.axis_index("tp")
    micro_rows = per_group * n_groups
    share = per_group // n_pairs
    gain = norm_gain[0]
    router_w = router[0]
    total_ids = router_w.shape[1]
    slot_count = max(2, (per_group * top_count + total_ids - 1) // total_ids)
    d_gate = dense_gate[0]
    d_up = dense_up[0]
    d_down = dense_down[0]
    e_gate = expert_gate[0, 0]
    e_up = expert_up[0, 0]
    e_down = expert_down[0, 0]
    slot_range = jnp.arange(slot_count, dtype=jnp.float32)
    incoming = jnp.zeros((per_group, width), jnp.bfloat16)
    outputs = jnp.zeros((n_micro, per_group, width), jnp.bfloat16)
    for tick_index in range(n_micro + 1):
        local_micro = tick_index - section
        micro_index = jnp.clip(local_micro, 0, n_micro - 1)
        valid = jnp.logical_and(local_micro >= 0, local_micro < n_micro)
        first_input = acts[min(tick_index, n_micro - 1)]
        current = jnp.where(section == 0, first_input, incoming)
        route_rows = lax.dynamic_index_in_dim(route_ids[0], micro_index, 0, keepdims=False)
        widened, normed = normalize(current, gain)
        weights, picked, zero_share = choice_weights(normed, route_rows, router_w, n_groups)
        all_normed = gathered_copies(normed, EP, 0)
        all_routes = gathered_copies(route_rows, EP, 0)
        blocks = all_normed.reshape(n_groups, per_group, width)
        mine = jnp.sum((all_routes == group_pos).astype(jnp.float32), axis=-1)
        column = lax.dynamic_slice_in_dim(router_w, group_pos, 1, 1)
        own_gate = jax.nn.sigmoid(jnp.dot(all_normed, column, preferred_element_type=jnp.float32))[
            :, 0
        ]
        hot = mine.reshape(n_groups, per_group)
        coef_rows = (own_gate * mine).reshape(n_groups, per_group)
        position = jnp.cumsum(hot, axis=1) - hot
        select = hot[:, None, :] * (position[:, None, :] == slot_range[None, :, None]).astype(
            jnp.float32
        )
        chosen = jnp.einsum(
            "bsi,bid->bsd", select.astype(jnp.bfloat16), blocks, preferred_element_type=jnp.float32
        ).astype(jnp.bfloat16)
        flat = chosen.reshape(-1, width)
        produced = gated_block(flat, e_gate, e_up, e_down).reshape(chosen.shape[:-1] + (width,))
        extra = jnp.einsum("bsi,bsd->bid", select * coef_rows[:, None, :], produced).reshape(
            micro_rows, width
        )
        summed = sum_in_two_steps(
            gated_block(all_normed, d_gate, d_up, d_down) + extra,
            (("ep_0", "ep_1"), ("ep_2", "tp")),
            0,
        )
        offset = pair_pos * share
        own_inputs = lax.dynamic_slice_in_dim(widened, offset, share, 0)
        own_normed = lax.dynamic_slice_in_dim(normed, offset, share, 0).astype(jnp.float32)
        own_zero = lax.dynamic_slice_in_dim(zero_share, offset, share, 0)
        result_part = (own_inputs + summed + own_zero[:, None] * own_normed).astype(jnp.bfloat16)
        finished = gathered_copies(result_part, "tp", 0)
        updated = lax.dynamic_update_index_in_dim(outputs, finished, micro_index, 0)
        outputs = jnp.where(valid, updated, outputs)
        if tick_index < n_micro:
            incoming = from_behind(finished, "pp", 1)
    return outputs[None]


def solution(mesh):
    finer = Mesh(
        mesh.devices.reshape(mesh.shape["pp"], 4, 4, 4, mesh.shape["tp"]),
        ("pp", "ep_0", "ep_1", "ep_2", "tp"),
    )
    in_specs = (
        P(None, EP, None),
        P("pp", None, EP, None),
        P("pp", None),
        P("pp", None, None),
        P("pp", None, EP_TP),
        P("pp", None, EP_TP),
        P("pp", EP_TP, None),
        P("pp", EP, None, "tp"),
        P("pp", EP, None, "tp"),
        P("pp", EP, "tp", None),
    )
    out_specs = P("pp", None, EP, None)
    return jax.shard_map(
        on_device, mesh=finer, in_specs=in_specs, out_specs=out_specs, check_vma=False
    )
```

profile of v0, /device:TPU:1, one launch (start us, length us, event | category | flops | bytes accessed | tf_op | source)
XLA Modules:
  0.0 866.7 jit_solution(18323345615448218824)
XLA Ops:
  1.6 12.5 %all-to-all-start.1 = ((s32[64,6,8]{2,1,0:T(8,128)}), s32[64,6,8]{2,1,0:T(8,128)S(1)}, u32[]{:S(2)}, u32[]{:S(2)}) async-start(s32[64,6,8]{2,1,0:T(8,128)} %broadcast_in_dim.81), calls=%async_computation.1 | async-start | bytes 524288 | tf_op jit(solution)/shard_map/all_to_all | solution.py:13
  17.5 7.7 all-to-all-done.1
  28.0 6.5 all-to-all-start
  34.8 71.0 %all-to-all-done = bf16[64,6,3072]{2,1,0:T(8,128)(2,1)} async-done(((bf16[64,6,3072]{2,1,0:T(8,128)(2,1)}), bf16[64,6,3072]{2,1,0:T(8,128)(2,1)}, u32[]{:S(2)}, u32[]{:S(2)}) %all-to-all-start) | async-done | bytes 2359328 | tf_op jit(solution)/shard_map/all_to_all | solution.py:13
  129.3 5.6 reshape.241
  138.0 7.3 convolution_add_fusion.2
  145.3 4.6 all-to-all-start.2
  151.6 104.4 %all-to-all-done.2 = f32[16,24,3072]{2,1,0:T(8,128)} async-done(((f32[16,24,3072]{2,1,0:T(8,128)}), f32[16,24,3072]{2,1,0:T(8,128)}, u32[]{:S(2)}, u32[]{:S(2)}) %all-to-all-start.2) | async-done | bytes 4718624 | tf_op jit(solution)/shard_map/all_to_all | solution.py:34
  261.2 10.1 %all-to-all-start.3 = ((f32[8,3,3072]{2,1,0:T(4,128)}), f32[8,3,3072]{2,1,0:T(4,128)}, u32[]{:S(2)}, u32[]{:S(2)}) async-start(f32[8,3,3072]{2,1,0:T(4,128)} %reshape.243), calls=%async_computation.3 | async-start | bytes 786432 | tf_op jit(solution)/shard_map/all_to_all | solution.py:34
  271.9 11.5 %all-to-all-done.3 = f32[8,3,3072]{2,1,0:T(4,128)} async-done(((f32[8,3,3072]{2,1,0:T(4,128)}), f32[8,3,3072]{2,1,0:T(4,128)}, u32[]{:S(2)}, u32[]{:S(2)}) %all-to-all-start.3) | async-done | bytes 294944 | tf_op jit(solution)/shard_map/all_to_all | solution.py:34
  285.5 9.2 %all_to_all.75 = bf16[2,3,3072]{2,1,0:T(4,128)(2,1)S(1)} all-to-all(bf16[2,3,3072]{2,1,0:T(4,128)(2,1)S(1)} %broadcast_in_dim.83), channel_id=1, replica_groups=mesh['pp'=2,'ep_0'=4,'ep_1'=4,'ep_2'=4,'tp'=2] {'tp'}, dimensions={0} | all-to-all | bytes 73728 | tf_op jit(solution)/shard_map/all_to_all | solution.py:13
  297.4 7.1 all-to-all-start.6
  306.4 8.5 all-to-all-done.6
  316.9 5.6 all-to-all-start.5
  323.7 68.6 %all-to-all-done.5 = bf16[64,6,3072]{2,1,0:T(8,128)(2,1)} async-done(((bf16[64,6,3072]{2,1,0:T(8,128)(2,1)}), bf16[64,6,3072]{2,1,0:T(8,128)(2,1)}, u32[]{:S(2)}, u32[]{:S(2)}) %all-to-all-start.5) | async-done | bytes 2359328 | tf_op jit(solution)/shard_map/all_to_all | solution.py:13
  418.5 4.6 fusion.20
  423.0 5.6 reshape.247
  428.6 7.3 convolution_add_fusion.1
  436.0 109.3 %all_to_all.76 = f32[16,24,3072]{2,1,0:T(8,128)} all-to-all(f32[16,24,3072]{2,1,0:T(8,128)} %bitcast.143), channel_id=1, replica_groups=mesh['pp'=2,'ep_0'=4,'ep_1'=4,'ep_2'=4,'tp'=2] {'ep_0','ep_1'}, dimensions={0} | all-to-all | bytes 9437184 | tf_op jit(solution)/shard_map/all_to_all | solution.py:34
  556.6 9.2 %all-to-all-done.8 = f32[8,3,3072]{2,1,0:T(4,128)} async-done(((f32[8,3,3072]{2,1,0:T(4,128)}), f32[8,3,3072]{2,1,0:T(4,128)}, u32[]{:S(2)}, u32[]{:S(2)}) %all-to-all-start.8) | async-done | bytes 294944 | tf_op jit(solution)/shard_map/all_to_all | solution.py:34
  568.5 9.8 %all_to_all.77 = bf16[2,3,3072]{2,1,0:T(4,128)(2,1)} all-to-all(bf16[2,3,3072]{2,1,0:T(4,128)(2,1)S(1)} %broadcast_in_dim.87), channel_id=1, replica_groups=mesh['pp'=2,'ep_0'=4,'ep_1'=4,'ep_2'=4,'tp'=2] {'tp'}, dimensions={0} | all-to-all | bytes 73728 | tf_op jit(solution)/shard_map/all_to_all | solution.py:13
  581.8 7.7 all-to-all-start.11
  591.3 8.6 all-to-all-done.11
  602.0 5.6 all-to-all-start.10
  608.8 68.4 %all-to-all-done.10 = bf16[64,6,3072]{2,1,0:T(8,128)(2,1)} async-done(((bf16[64,6,3072]{2,1,0:T(8,128)(2,1)}), bf16[64,6,3072]{2,1,0:T(8,128)(2,1)}, u32[]{:S(2)}, u32[]{:S(2)}) %all-to-all-start.10) | async-done | bytes 2359328 | tf_op jit(solution)/shard_map/all_to_all | solution.py:13
  707.3 5.6 reshape.253
  712.9 7.3 convolution_add_fusion
  720.2 4.7 all-to-all-start.12
  725.6 105.3 %all-to-all-done.12 = f32[16,24,3072]{2,1,0:T(8,128)} async-done(((f32[16,24,3072]{2,1,0:T(8,128)}), f32[16,24,3072]{2,1,0:T(8,128)}, u32[]{:S(2)}, u32[]{:S(2)}) %all-to-all-start.12) | async-done | bytes 4718624 | tf_op jit(solution)/shard_map/all_to_all | solution.py:34
  834.4 4.6 all-to-all-start.13
  844.2 5.7 all-to-all-done.13
  852.1 6.2 all-to-all-start.14
  (158 shorter events, 150.6 us)
Async XLA Ops:
  0.0 125.2 %copy-start = (bf16[1,1,512,3072]{3,2,1,0:T(8,128)(2,1)S(1)}, bf16[1,1,512,3072]{3,2,1,0:T(8,128)(2,1)}, u32[]{:S(2)}) copy-start(bf16[1,1,512,3072]{3,2,1,0:T(8,128)(2,1)} %param.19) | copy-start | bytes 9437188
  1.6 23.5 %all-to-all-start.1 = ((s32[64,6,8]{2,1,0:T(8,128)}), s32[64,6,8]{2,1,0:T(8,128)S(1)}, u32[]{:S(2)}, u32[]{:S(2)}) async-start(s32[64,6,8]{2,1,0:T(8,128)} %broadcast_in_dim.81), calls=%async_computation.1 | async-start | bytes 524288 | tf_op jit(solution)/shard_map/all_to_all | solution.py:13
  28.0 77.8 %all-to-all-start = ((bf16[64,6,3072]{2,1,0:T(8,128)(2,1)}), bf16[64,6,3072]{2,1,0:T(8,128)(2,1)}, u32[]{:S(2)}, u32[]{:S(2)}) async-start(bf16[64,6,3072]{2,1,0:T(8,128)(2,1)} %broadcast_in_dim.80), calls=%async_computation | async-start | bytes 6291456 | tf_op jit(solution)/shard_map/all_to_all | solution.py:13
  119.6 2.9 copy-start.1
  119.6 3.3 copy-start.12
  129.3 8.7 %copy-start.4 = (bf16[1,48,3072]{2,1,0:T(8,128)(2,1)S(1)}, bf16[1,48,3072]{2,1,0:T(8,128)(2,1)}, u32[]{:S(2)}) copy-start(bf16[1,48,3072]{2,1,0:T(8,128)(2,1)} %param.16) | copy-start | bytes 884740
  145.3 110.7 %all-to-all-start.2 = ((f32[16,24,3072]{2,1,0:T(8,128)}), f32[16,24,3072]{2,1,0:T(8,128)}, u32[]{:S(2)}, u32[]{:S(2)}) async-start(f32[16,24,3072]{2,1,0:T(8,128)} %bitcast.141), calls=%async_computation.2 | async-start | bytes 9437184 | tf_op jit(solution)/shard_map/all_to_all | solution.py:34
  261.2 22.3 %all-to-all-start.3 = ((f32[8,3,3072]{2,1,0:T(4,128)}), f32[8,3,3072]{2,1,0:T(4,128)}, u32[]{:S(2)}, u32[]{:S(2)}) async-start(f32[8,3,3072]{2,1,0:T(4,128)} %reshape.243), calls=%async_computation.3 | async-start | bytes 786432 | tf_op jit(solution)/shard_map/all_to_all | solution.py:34
  294.7 11.5 %copy-start.8 = (bf16[2,3,3072]{2,1,0:T(4,128)(2,1)}, bf16[2,3,3072]{2,1,0:T(4,128)(2,1)S(1)}, u32[]{:S(2)}) copy-start(bf16[2,3,3072]{2,1,0:T(4,128)(2,1)S(1)} %all_to_all.75) | copy-start | bytes 110596
  295.4 9.2 %collective-permute-start = (bf16[6,3072]{1,0:T(8,128)(2,1)}, bf16[6,3072]{1,0:T(8,128)(2,1)}, u32[]{:S(2)}, u32[]{:S(2)}) collective-permute-start(bf16[6,3072]{1,0:T(8,128)(2,1)} %reshape.244), channel_id=1, source_target_pairs={{0,128},{1,129},{2,130},{3,131},{4,132},{5,133},{6,134},{7,135},{8... | collective-permute-start | bytes 110600 | tf_op jit(solution)/shard_map/ppermute | solution.py:46
  297.4 17.5 %all-to-all-start.6 = ((s32[64,6,8]{2,1,0:T(8,128)}), s32[64,6,8]{2,1,0:T(8,128)}, u32[]{:S(2)}, u32[]{:S(2)}) async-start(s32[64,6,8]{2,1,0:T(8,128)} %broadcast_in_dim.86), calls=%async_computation.6 | async-start | bytes 524288 | tf_op jit(solution)/shard_map/all_to_all | solution.py:13
  306.3 10.6 %copy-start.7 = (bf16[6,3072]{1,0:T(8,128)(2,1)}, bf16[6,3072]{1,0:T(8,128)(2,1)S(1)}, u32[]{:S(2)}) copy-start(bf16[6,3072]{1,0:T(8,128)(2,1)S(1)} %multiply_convert_fusion.1) | copy-start | bytes 110596
  316.9 75.4 %all-to-all-start.5 = ((bf16[64,6,3072]{2,1,0:T(8,128)(2,1)}), bf16[64,6,3072]{2,1,0:T(8,128)(2,1)}, u32[]{:S(2)}, u32[]{:S(2)}) async-start(bf16[64,6,3072]{2,1,0:T(8,128)(2,1)} %broadcast_in_dim.85), calls=%async_computation.5 | async-start | bytes 6291456 | tf_op jit(solution)/shard_map/all_to_all | solution.py:13
  409.2 2.9 copy-start.2
  409.2 3.3 copy-start.13
  423.0 5.6 copy-start.10
  548.5 41.0 %copy-start.5 = (bf16[1,6,3072]{2,0,1:T(2,128)(2,1)S(1)}, bf16[1,6,3072]{2,0,1:T(2,128)(2,1)}, u32[]{:S(2)}) copy-start(bf16[1,6,3072]{2,0,1:T(2,128)(2,1)} %get-tuple-element.9) | copy-start | bytes 110596
  550.4 15.5 %all-to-all-start.8 = ((f32[8,3,3072]{2,1,0:T(4,128)}), f32[8,3,3072]{2,1,0:T(4,128)}, u32[]{:S(2)}, u32[]{:S(2)}) async-start(f32[8,3,3072]{2,1,0:T(4,128)} %reshape.249), calls=%async_computation.8 | async-start | bytes 786432 | tf_op jit(solution)/shard_map/all_to_all | solution.py:34
  579.8 9.8 %collective-permute-start.1 = (bf16[6,3072]{1,0:T(8,128)(2,1)}, bf16[6,3072]{1,0:T(8,128)(2,1)}, u32[]{:S(2)}, u32[]{:S(2)}) collective-permute-start(bf16[6,3072]{1,0:T(8,128)(2,1)} %reshape.250), channel_id=1, source_target_pairs={{0,128},{1,129},{2,130},{3,131},{4,132},{5,133},{6,134},{7,135},{8... | collective-permute-start | bytes 110600 | tf_op jit(solution)/shard_map/ppermute | solution.py:46
  581.8 18.1 %all-to-all-start.11 = ((s32[64,6,8]{2,1,0:T(8,128)}), s32[64,6,8]{2,1,0:T(8,128)}, u32[]{:S(2)}, u32[]{:S(2)}) async-start(s32[64,6,8]{2,1,0:T(8,128)} %broadcast_in_dim.91), calls=%async_computation.11 | async-start | bytes 524288 | tf_op jit(solution)/shard_map/all_to_all | solution.py:13
  591.3 10.7 %copy-start.6 = (bf16[6,3072]{1,0:T(8,128)(2,1)}, bf16[6,3072]{1,0:T(8,128)(2,1)S(1)}, u32[]{:S(2)}) copy-start(bf16[6,3072]{1,0:T(8,128)(2,1)S(1)} %multiply_convert_fusion) | copy-start | bytes 110596
  602.0 75.2 %all-to-all-start.10 = ((bf16[64,6,3072]{2,1,0:T(8,128)(2,1)}), bf16[64,6,3072]{2,1,0:T(8,128)(2,1)}, u32[]{:S(2)}, u32[]{:S(2)}) async-start(bf16[64,6,3072]{2,1,0:T(8,128)(2,1)} %broadcast_in_dim.90), calls=%async_computation.10 | async-start | bytes 6291456 | tf_op jit(solution)/shard_map/all_to_all | solution.py:13
  694.1 2.9 copy-start.3
  694.1 3.3 copy-start.14
  707.3 5.6 copy-start.11
  720.2 4.7 copy-start.9
  720.2 110.7 %all-to-all-start.12 = ((f32[16,24,3072]{2,1,0:T(8,128)}), f32[16,24,3072]{2,1,0:T(8,128)}, u32[]{:S(2)}, u32[]{:S(2)}) async-start(f32[16,24,3072]{2,1,0:T(8,128)} %bitcast.142), calls=%async_computation.12 | async-start | bytes 9437184 | tf_op jit(solution)/shard_map/all_to_all | solution.py:34
  834.4 15.5 %all-to-all-start.13 = ((f32[8,3,3072]{2,1,0:T(4,128)}), f32[8,3,3072]{2,1,0:T(4,128)S(1)}, u32[]{:S(2)}, u32[]{:S(2)}) async-start(f32[8,3,3072]{2,1,0:T(4,128)} %reshape.255), calls=%async_computation.13 | async-start | bytes 786432 | tf_op jit(solution)/shard_map/all_to_all | solution.py:34
  852.1 13.0 %all-to-all-start.14 = ((bf16[2,3,3072]{2,1,0:T(4,128)(2,1)}), bf16[2,3,3072]{2,1,0:T(4,128)(2,1)S(1)}, u32[]{:S(2)}, u32[]{:S(2)}) async-start(bf16[2,3,3072]{2,1,0:T(4,128)(2,1)} %broadcast_in_dim.92), calls=%async_computation.14 | async-start | bytes 98304 | tf_op jit(solution)/shard_map/all_to_all | solution.py:13
where the time goes:
time: 871 us; the launch traced here: 867 us
  waiting for transfers between devices  473 us (54%)
  blocking collectives  128 us (15%)
  matrix products  84 us (10%)
  starting transfers between devices  82.2 us (9%)
  local copies, waits for them, and re-layouts  73.8 us (8%)
  other arithmetic  24.6 us (3%)
    all_to_all x7, waiting for transfers between devices, sent_to_all(): return lax.all_to_all(copies, axis, split_axis=0, concat_axis=0, tiled=True)  237 us
    all_to_all x5, waiting for transfers between devices, sum_at_owner(): lax.all_to_all(in_blocks(shard, dim, length), axis, 0, 0, tiled=True)  236 us
    all_to_all x1, blocking collectives, sum_at_owner(): lax.all_to_all(in_blocks(shard, dim, length), axis, 0, 0, tiled=True)  109 us
    all_to_all x7, starting transfers between devices, sent_to_all(): return lax.all_to_all(copies, axis, split_axis=0, concat_axis=0, tiled=True)  51.3 us
    all_to_all x5, starting transfers between devices, sum_at_owner(): lax.all_to_all(in_blocks(shard, dim, length), axis, 0, 0, tiled=True)  28.4 us
    dot_general x6, matrix products, gated_block(): return jnp.dot(hidden, w_down, preferred_element_type=jnp.float32)  27.3 us
    all_to_all x2, blocking collectives, sent_to_all(): return lax.all_to_all(copies, axis, split_axis=0, concat_axis=0, tiled=True)  19 us
    dot_general x6, matrix products, gated_block(): gate_part = jnp.dot(inputs, w_gate, preferred_element_type=jnp.float32)  17.9 us
  transfers between devices with their start and end apart: 14, of which 12 were waited for; matrix products, arithmetic and copies ran while one was open for 3% of the time, Pallas kernels for 0%

commit v1 on v0

v1 whole, which is shorter than its diff:
```python
import functools

import jax
import jax.numpy as jnp
from jax import lax
from jax.experimental import pallas as pl
from jax.experimental.pallas import tpu as pltpu
from jax.sharding import Mesh
from jax.sharding import PartitionSpec as P

MESH = pl.DeviceIdType.MESH
EP = ("ep_0", "ep_1", "ep_2")
EP_TP = ("ep_0", "ep_1", "ep_2", "tp")
F32 = jnp.float32
BF16 = jnp.bfloat16
ROWS = 8
LANES = 128


def kernel(cfg, *refs):
    (acts, routes, gain, router_h, dg_h, du_h, dd_h, eg_h, eu_h, ed_h, out) = refs[:11]
    (G, PT, R1, S1, R2, S2, R3, TS, TR, X, OB, CODE, MASK, ZS) = refs[11:25]
    (RT, DG, DU, EG, EU, ED, W1, LH, DN, CH) = refs[25:35]
    (w_sem, ag_s, ag_r, rs_s, rs_r, tp_s, tp_r, pp_s, pp_r) = refs[35:]
    sizes, n_tp, width, n_micro, n_tok, topk, n_real, n_total, slots, chunk = cfg
    n_blocks = sizes[0] * sizes[1] * sizes[2]
    rows = n_blocks * ROWS
    n_slots = n_blocks * slots
    part = width // 3
    offs = (0, part, 2 * part)
    gw = (part, part, part + LANES)
    order = ((0, 1, 2), (1, 2, 0), (2, 0, 1))

    sec = lax.axis_index("pp")
    me = tuple(lax.axis_index(a) for a in EP)
    tp = lax.axis_index("tp")
    group = (me[0] * sizes[1] + me[1]) * sizes[2] + me[2]

    def peer(axis, o):
        n = sizes[axis]
        if axis != 1:
            return {EP[axis]: lax.rem(me[axis] + o + n, n)}
        step = o if abs(o) <= n // 2 else o - n * (o // abs(o))
        z = lax.rem(tp * n + me[1] + step + n * n_tp, n * n_tp)
        return {"ep_1": lax.rem(z, n), "tp": z // n}

    far = {"tp": 1 - tp}
    above = {"pp": 1 - sec}

    def weight_copies():
        pairs = ((router_h.at[0], RT), (dg_h.at[0], DG), (du_h.at[0], DU), (dd_h.at[0], DN.at[pl.ds(0, dd_h.shape[1])]),
                 (eg_h.at[0, 0], EG), (eu_h.at[0, 0], EU), (ed_h.at[0, 0], ED))
        return [pltpu.make_async_copy(s, d, w_sem.at[i]) for i, (s, d) in enumerate(pairs)]

    for c in weight_copies():
        c.start()

    X[...] = jnp.zeros_like(X)
    barrier = pltpu.get_barrier_semaphore()
    greeted = 0
    for axis in range(3):
        for o in range(1, sizes[axis]):
            pl.semaphore_signal(barrier, inc=1, device_id=peer(axis, -o), device_id_type=MESH)
            greeted += 1
    for who in (far, above):
        pl.semaphore_signal(barrier, inc=1, device_id=who, device_id_type=MESH)
        greeted += 1

    CODE[...] = jnp.zeros_like(CODE)
    MASK[...] = jnp.zeros_like(MASK)
    W1[...] = jnp.zeros_like(W1)
    DN[pl.ds(dd_h.shape[1], LANES - dd_h.shape[1])] = jnp.zeros((LANES - dd_h.shape[1], width), BF16)
    for m in range(n_micro):
        ids = routes[0, m]
        lane = lax.broadcasted_iota(jnp.int32, (n_tok, LANES), 1)
        named = jnp.zeros((n_tok, LANES), F32)
        for k in range(topk):
            named += (ids[:, k : k + 1] == lane).astype(F32)
        MASK[m, 0:n_tok] = named
        before = jnp.zeros((1, LANES), F32)
        for t in range(n_tok):
            row = named[t : t + 1]
            CODE[m, t : t + 1] = row * (before + 1.0)
            before += row

    pl.semaphore_wait(barrier, greeted)

    def ag_copy(m, p, s, o):
        axes = order[p]
        at = [me[0], me[1], me[2]]
        for a in axes[:s]:
            at[a] = slice(None)
        ref = G.at[m, at[0], at[1], at[2], :, pl.ds(offs[p], gw[p])]
        return pltpu.make_async_remote_copy(
            src_ref=ref, dst_ref=ref, send_sem=ag_s.at[m, p, s, o - 1], recv_sem=ag_r.at[m, p, s, o - 1],
            device_id=peer(axes[s], o), device_id_type=MESH)

    def ag_start(m, p, s):
        for o in range(1, sizes[order[p][s]]):
            ag_copy(m, p, s, o).start()

    def ag_wait(m, p, s):
        for o in range(1, sizes[order[p][s]]):
            ag_copy(m, p, s, o).wait_recv()

    def rs_refs(m, p, s, o):
        axis = order[p][2 - s]
        there = lax.rem(me[axis] + o, sizes[axis])
        if s == 0:
            at = [slice(None)] * 3
            at[axis] = there
            return PT.at[m, at[0], at[1], at[2], :, pl.ds(offs[p], part)], R1.at[m, p, o - 1]
        if s == 1:
            rest = [d for d in range(3) if d != order[p][2]]
            at = [slice(None)] * 2
            at[rest.index(axis)] = there
            return S1.at[m, p, at[0], at[1]], R2.at[m, p, o - 1]
        return S2.at[m, p, there], R3.at[m, p, o - 1]

    def rs_copy(m, p, s, o):
        src, dst = rs_refs(m, p, s, o)
        return pltpu.make_async_remote_copy(
            src_ref=src, dst_ref=dst, send_sem=rs_s.at[m, p, s, o - 1], recv_sem=rs_r.at[m, p, s, o - 1],
            device_id=peer(order[p][2 - s], o), device_id_type=MESH)

    def rs_start(m, p, s):
        for o in range(1, sizes[order[p][2 - s]]):
            rs_copy(m, p, s, o).start()

    def rs_wait(m, p, s):
        for o in range(1, sizes[order[p][2 - s]]):
            rs_copy(m, p, s, o).wait_recv()

    def tp_copy(m):
        return pltpu.make_async_remote_copy(
            src_ref=TS.at[m], dst_ref=TR.at[m], send_sem=tp_s.at[m], recv_sem=tp_r.at[m],
            device_id=far, device_id_type=MESH)

    def pp_copy(m):
        return pltpu.make_async_remote_copy(
            src_ref=OB.at[m], dst_ref=X.at[m], send_sem=pp_s.at[m], recv_sem=pp_r.at[m],
            device_id=above, device_id_type=MESH)

    def take_input(m):
        @pl.when(sec == 0)
        def _():
            X[m, 0:n_tok] = acts[m]

        @pl.when(sec == 1)
        def _():
            pp_copy(m).wait_recv()

    def norm_and_send(m):
        wide = X[m].astype(F32)
        spread = jnp.mean(wide * wide, axis=-1, keepdims=True)
        normed = (wide * lax.rsqrt(spread + 1e-06) * gain[...].astype(F32)).astype(BF16)
        G[m, me[0], me[1], me[2], :, pl.ds(0, width)] = normed
        G[m, me[0], me[1], me[2], :, pl.ds(width, LANES)] = CODE[m].astype(BF16)
        for p in range(3):
            ag_start(m, p, 0)

    def zero_share(m):
        normed = G[m, me[0], me[1], me[2], :, pl.ds(0, width)]
        gates = jax.nn.sigmoid(jnp.dot(normed, RT[...], preferred_element_type=F32))
        lane = lax.broadcasted_iota(jnp.int32, gates.shape, 1)
        share = jnp.where(lane >= n_real, MASK[m][:, :n_total] * gates, 0.0)
        ZS[m] = jnp.broadcast_to(jnp.sum(share, axis=-1, keepdims=True), (ROWS, LANES))

    def tokens(m, start, size):
        return G[m, :, :, :, :, pl.ds(start, size)].reshape(rows, size)

    def compute(m):
        hid = jnp.zeros((rows, 2 * LANES), F32)
        for p in range(3):
            hid += jnp.dot(tokens(m, offs[p], part), W1[pl.ds(offs[p], part)], preferred_element_type=F32)
        LH[:, 0:LANES] = (jax.nn.silu(hid[:, :LANES]) * hid[:, LANES:]).astype(BF16)
        codes = tokens(m, width, LANES)
        pick = (lax.broadcasted_iota(jnp.int32, (LANES, n_slots), 0) == group).astype(BF16)
        col = jnp.dot(codes, pick, preferred_element_type=F32)
        tok = lax.broadcasted_iota(jnp.int32, (rows, n_slots), 0)
        slot = lax.broadcasted_iota(jnp.int32, (rows, n_slots), 1)
        hit = (tok // ROWS == slot // slots) & (col == (slot % slots + 1).astype(F32))
        LH[:, LANES:] = jnp.where(hit, 1.0, 0.0).astype(BF16)
        pick_t = (lax.broadcasted_iota(jnp.int32, (ROWS, LANES), 1) == group).astype(BF16)
        row = lax.dot_general(pick_t, codes, (((1,), (1,)), ((), ())), preferred_element_type=F32)[0:1]
        slot = lax.broadcasted_iota(jnp.int32, (n_slots, rows), 0)
        tok = lax.broadcasted_iota(jnp.int32, (n_slots, rows), 1)
        hit = (tok // ROWS == slot // slots) & (row == (slot % slots + 1).astype(F32))
        chooser = jnp.where(hit, 1.0, 0.0).astype(BF16)
        for c in range(0, width, chunk):
            CH[:, pl.ds(c, chunk)] = jnp.dot(chooser, tokens(m, c, chunk), preferred_element_type=F32).astype(BF16)
        chosen = CH[...]
        logit = jnp.dot(chosen, RT[...], preferred_element_type=F32)
        lane = lax.broadcasted_iota(jnp.int32, logit.shape, 1)
        coef = jax.nn.sigmoid(jnp.sum(jnp.where(lane == group, logit, 0.0), axis=-1, keepdims=True))
        gate = jnp.dot(chosen, EG[...], preferred_element_type=F32)
        up = jnp.dot(chosen, EU[...], preferred_element_type=F32)
        inner = (jax.nn.silu(gate) * up).astype(BF16)
        for c in range(0, width, chunk):
            made = jnp.dot(inner, ED[:, pl.ds(c, chunk)], preferred_element_type=F32)
            DN[pl.ds(LANES, n_slots), pl.ds(c, chunk)] = (coef * made).astype(BF16)
        for p in range(3):
            for c in range(offs[p], offs[p] + part, chunk):
                both = jnp.dot(LH[...], DN[:, pl.ds(c, chunk)], preferred_element_type=F32).astype(BF16)
                PT[m, :, :, :, :, pl.ds(c, chunk)] = both.reshape(*sizes, ROWS, chunk)
            rs_start(m, p, 0)

    def rs_sum(m, p, s):
        axis = order[p][2 - s]
        n = sizes[axis]
        if s == 0:
            rest = [d for d in range(3) if d != axis]

            def add(i, carry):
                at = [slice(None)] * 3
                at[axis] = me[axis]
                at[rest[0]] = i
                total = PT[m, at[0], at[1], at[2], :, pl.ds(offs[p], part)].astype(F32)
                for o in range(n - 1):
                    total += R1[m, p, o, i].astype(F32)
                S1[m, p, i] = total.astype(BF16)
                return carry

            lax.fori_loop(0, sizes[rest[0]], add, 0)
        elif s == 1:
            rest = [d for d in range(3) if d != order[p][2]]
            at = [slice(None)] * 2
            at[rest.index(axis)] = me[axis]
            total = S1[m, p, at[0], at[1]].astype(F32)
            for o in range(n - 1):
                total += R2[m, p, o].astype(F32)
            S2[m, p] = total.astype(BF16)
        else:
            total = S2[m, p, me[axis]].astype(F32)
            for o in range(n - 1):
                total += R3[m, p, o].astype(F32)
            TS[m, :, pl.ds(offs[p], part)] = total.astype(BF16)

    def finish(m):
        tp_copy(m).wait_recv()
        normed = G[m, me[0], me[1], me[2], :, pl.ds(0, width)].astype(F32)
        summed = TS[m].astype(F32) + TR[m].astype(F32)
        done = (X[m].astype(F32) + summed + ZS[m][:, 0:1] * normed).astype(BF16)
        OB[m] = done
        out[0, m] = done[0:n_tok]

        @pl.when(sec == 0)
        def _():
            pp_copy(m).start()

    for m in range(n_micro):
        take_input(m)
        norm_and_send(m)
        if m == 0:
            for c in weight_copies():
                c.wait()
            W1[:, 0 : DG.shape[1]] = DG[...]
            W1[:, LANES : LANES + DU.shape[1]] = DU[...]
        zero_share(m)
        for s in range(3):
            for p in range(3):
                ag_wait(m, p, s)
                if s < 2:
                    ag_start(m, p, s + 1)
        compute(m)
        for s in range(3):
            for p in range(3):
                rs_wait(m, p, s)
                rs_sum(m, p, s)
                if s < 2:
                    rs_start(m, p, s + 1)
        tp_copy(m).start()
        finish(m)

    for m in range(n_micro):
        for p in range(3):
            for s in range(3):
                for o in range(1, sizes[order[p][s]]):
                    ag_copy(m, p, s, o).wait_send()
                for o in range(1, sizes[order[p][2 - s]]):
                    rs_copy(m, p, s, o).wait_send()
        tp_copy(m).wait_send()

        @pl.when(sec == 0)
        def _():
            pp_copy(m).wait_send()


def on_device(sizes, n_tp, acts, routes, gain, router, dg, du, dd, eg, eu, ed):
    n_micro, n_tok, width = acts.shape
    topk = routes.shape[-1]
    n_total = router.shape[-1]
    n_blocks = sizes[0] * sizes[1] * sizes[2]
    slots = max(2, (n_tok * topk + n_total - 1) // n_total)
    n_slots = n_blocks * slots
    part = width // 3
    chunk = min(512, part)
    n = sizes[0]
    inner = eg.shape[-1]
    cfg = (sizes, n_tp, width, n_micro, n_tok, topk, n_blocks, n_total, slots, chunk)
    vm = pltpu.VMEM
    scratch = [
        vm((n_micro, *sizes, ROWS, width + LANES), BF16),
        vm((n_micro, *sizes, ROWS, width), BF16),
        vm((n_micro, 3, n - 1, n, n, ROWS, part), BF16),
        vm((n_micro, 3, n, n, ROWS, part), BF16),
        vm((n_micro, 3, n - 1, n, ROWS, part), BF16),
        vm((n_micro, 3, n, ROWS, part), BF16),
        vm((n_micro, 3, n - 1, ROWS, part), BF16),
        vm((n_micro, ROWS, width), BF16),
        vm((n_micro, ROWS, width), BF16),
        vm((n_micro, ROWS, width), BF16),
        vm((n_micro, ROWS, width), BF16),
        vm((n_micro, ROWS, LANES), F32),
        vm((n_micro, ROWS, LANES), F32),
        vm((n_micro, ROWS, LANES), F32),
        vm((width, n_total), BF16),
        vm((width, dg.shape[-1]), BF16),
        vm((width, du.shape[-1]), BF16),
        vm((width, inner), BF16),
        vm((width, inner), BF16),
        vm((inner, width), BF16),
        vm((width, 2 * LANES), BF16),
        vm((n_blocks * ROWS, LANES + n_slots), BF16),
        vm((LANES + n_slots, width), BF16),
        vm((n_slots, width), BF16),
        pltpu.SemaphoreType.DMA((7,)),
        pltpu.SemaphoreType.DMA((n_micro, 3, 3, n - 1)),
        pltpu.SemaphoreType.DMA((n_micro, 3, 3, n - 1)),
        pltpu.SemaphoreType.DMA((n_micro, 3, 3, n - 1)),
        pltpu.SemaphoreType.DMA((n_micro, 3, 3, n - 1)),
        pltpu.SemaphoreType.DMA((n_micro,)),
        pltpu.SemaphoreType.DMA((n_micro,)),
        pltpu.SemaphoreType.DMA((n_micro,)),
        pltpu.SemaphoreType.DMA((n_micro,)),
    ]
    in_vmem = pl.BlockSpec(memory_space=pltpu.VMEM)
    left = pl.BlockSpec(memory_space=pl.ANY)
    return pl.pallas_call(
        functools.partial(kernel, cfg),
        out_shape=jax.ShapeDtypeStruct((1, n_micro, n_tok, width), BF16),
        in_specs=[in_vmem] * 3 + [left] * 7,
        out_specs=in_vmem,
        scratch_shapes=scratch,
        compiler_params=pltpu.CompilerParams(
            collective_id=0, has_side_effects=True, vmem_limit_bytes=60 * 1024 * 1024
        ),
        name="relay",
    )(acts, routes, gain, router, dg, du, dd, eg, eu, ed)


def solution(mesh):
    n_tp = mesh.shape["tp"]
    side = round(mesh.shape["ep"] ** (1 / 3))
    sizes = (side, side, side)
    finer = Mesh(
        mesh.devices.reshape(mesh.shape["pp"], *sizes, n_tp),
        ("pp", "ep_0", "ep_1", "ep_2", "tp"),
    )
    in_specs = (
        P(None, EP, None),
        P("pp", None, EP, None),
        P("pp", None),
        P("pp", None, None),
        P("pp", None, EP_TP),
        P("pp", None, EP_TP),
        P("pp", EP_TP, None),
        P("pp", EP, None, "tp"),
        P("pp", EP, None, "tp"),
        P("pp", EP, "tp", None),
    )
    return jax.shard_map(
        functools.partial(on_device, sizes, n_tp),
        mesh=finer,
        in_specs=in_specs,
        out_specs=P("pp", None, EP, None),
        check_vma=False,
    )
```

time: 871 us -> 195 us (0.22)
  waiting for transfers between devices: 473 us -> 0 us
  Pallas kernels: 0 us -> 183 us
  blocking collectives: 128 us -> 0 us
  matrix products: 84 us -> 0 us
  starting transfers between devices: 82.2 us -> 0 us
  local copies, waits for them, and re-layouts: 73.8 us -> 10.9 us
  other arithmetic: 24.6 us -> 0 us
    all_to_all x12 -> x0, waiting for transfers between devices: 473 us -> none  [the longest x7 237 us: sent_to_all(): return lax.all_to_all(copies, axis, split_axis=0, concat_axis=0, tiled=True)]
    pallas_call x0 -> x1, Pallas kernels: none -> 183 us  [on_device(): pl.pallas_call(functools.partial(kernel, cfg), out_shape=jax.ShapeDtypeSt...]
    all_to_all x3 -> x0, blocking collectives: 128 us -> none  [the longest x1 109 us: sum_at_owner(): lax.all_to_all(in_blocks(shard, dim, length), axis, 0, 0, tiled=True)]
    dot_general x27 -> x0, matrix products: 84 us -> none  [the longest x6 27.3 us: gated_block(): return jnp.dot(hidden, w_down, preferred_element_type=jnp.float32)]
    all_to_all x12 -> x0, starting transfers between devices: 79.7 us -> none  [the longest x7 51.3 us: sent_to_all(): return lax.all_to_all(copies, axis, split_axis=0, concat_axis=0, tiled=True)]
    reshape x14 -> x0, local copies, waits for them, and re-layouts: 45.5 us -> none  [the longest x3 16.8 us: on_device(): jnp.einsum('bsi,bsd->bid', select * coef_rows[:, None, :], produced)]
    reduce_sum x18 -> x0, other arithmetic: 13.9 us -> none  [the longest x6 12.6 us: sum_at_owner(): return jnp.sum(tiles, axis=0)]
    broadcast_in_dim x12 -> x0, local copies, waits for them, and re-layouts: 12 us -> none  [the longest x9 9.84 us: sent_to_all(): copies = jnp.broadcast_to(shard, (lax.axis_size(axis), *shard.shape))]
  transfers between devices with their start and end apart: 14 -> 0, of which waited for: 12 -> 0; matrix products, arithmetic and copies ran while one was open for 3% -> 0% of each run, Pallas kernels for 0% -> 0%
where the time goes in v1:
time: 195 us; the launch traced here: 194 us
  Pallas kernels  183 us (94%)
  local copies, waits for them, and re-layouts  10.9 us (6%)
    pallas_call x1, Pallas kernels, on_device(): pl.pallas_call(functools.partial(kernel, cfg), out_shape=jax.ShapeDtypeSt...  183 us
    unnamed x5, local copies, waits for them, and re-layouts  9.32 us

profile of v1, /device:TPU:1, one launch (start us, length us, event | category | flops | bytes accessed | tf_op | source)
XLA Modules:
  0.0 193.5 jit_solution(5451066683456987414)
XLA Ops:
  0.0 1.3 copy.12.refs_1_
  1.3 1.5 copy.11.refs_0_
  2.8 2.2 %copy.13.refs_3_ = bf16[1,3072,96]{2,1,0:T(8,128)(2,1)} copy(bf16[1,3072,96]{1,2,0:T(8,128)(2,1)} %param.13) | data formatting | bytes 1179648 | tf_op args[3]
  5.0 2.1 %copy.14.refs_4_ = bf16[1,3072,48]{2,1,0:T(8,128)(2,1)} copy(bf16[1,3072,48]{1,2,0:T(8,128)(2,1)} %param.14) | data formatting | bytes 589824 | tf_op args[4]
  7.2 2.1 %copy.15.refs_5_ = bf16[1,3072,48]{2,1,0:T(8,128)(2,1)} copy(bf16[1,3072,48]{1,2,0:T(8,128)(2,1)} %param.15) | data formatting | bytes 589824 | tf_op args[5]
  9.3 182.6 %relay.1 = bf16[1,2,6,3072]{3,2,1,0:T(8,128)(2,1)} custom-call(bf16[2,6,3072]{2,1,0:T(8,128)(2,1)} %copy.11.refs_0_, s32[1,2,6,8]{3,2,1,0:T(8,128)} %copy.12.refs_1_, bf16[1,3072]{1,0:T(2,128)(2,1)} %refs_2_.1, bf16[1,3072,96]{2,1,0:T(8,128)(2,1)} %copy.13.refs_3_, bf16[1,3072,48]{2,1,0:T(8,128)(2,1)} %copy.14.refs_4_, bf16[1,3072,48]{2,1,0:T(8,128)(2,1)} %copy.15.refs_5_, ...), custom_call_target="tpu_custom_call" | custom-call | tf_op jit(solution)/shard_map/relay/pallas_call | solution.py:339
  191.9 1.6 copy.16

commit v2 on v1

--- a/solution.py
+++ b/solution.py
@@ -17,11 +17,15 @@
 LANES = 128
 
 
+def dot_t(a, b):
+    return lax.dot_general(a, b, (((1,), (1,)), ((), ())), preferred_element_type=F32)
+
+
 def kernel(cfg, *refs):
     (acts, routes, gain, router_h, dg_h, du_h, dd_h, eg_h, eu_h, ed_h, out) = refs[:11]
-    (G, PT, R1, S1, R2, S2, R3, TS, TR, X, OB, CODE, MASK, ZS) = refs[11:25]
-    (RT, DG, DU, EG, EU, ED, W1, LH, DN, CH) = refs[25:35]
-    (w_sem, ag_s, ag_r, rs_s, rs_r, tp_s, tp_r, pp_s, pp_r) = refs[35:]
+    (G, PT, RA, RB, S1, R2, S2, R3, TS, TR, X, OB, CODE, MASK, ZS) = refs[11:26]
+    (RT, EG, EU, ED, W1, LH, DN, CH) = refs[26:34]
+    (w_sem, ag_s, ag_r, rs_s, rs_r, fa_s, fa_r, fr_s, fr_r, tp_s, tp_r, pp_s, pp_r) = refs[34:]
     sizes, n_tp, width, n_micro, n_tok, topk, n_real, n_total, slots, chunk = cfg
     n_blocks = sizes[0] * sizes[1] * sizes[2]
     rows = n_blocks * ROWS
@@ -48,7 +52,9 @@
     above = {"pp": 1 - sec}
 
     def weight_copies():
-        pairs = ((router_h.at[0], RT), (dg_h.at[0], DG), (du_h.at[0], DU), (dd_h.at[0], DN.at[pl.ds(0, dd_h.shape[1])]),
+        hidden = dg_h.shape[1]
+        pairs = ((router_h.at[0], RT), (dg_h.at[0], W1.at[pl.ds(0, hidden)]), (du_h.at[0], W1.at[pl.ds(LANES, hidden)]),
+                 (dd_h.at[0], DN.at[pl.ds(0, hidden)]),
                  (eg_h.at[0, 0], EG), (eu_h.at[0, 0], EU), (ed_h.at[0, 0], ED))
         return [pltpu.make_async_copy(s, d, w_sem.at[i]) for i, (s, d) in enumerate(pairs)]
 
@@ -68,10 +74,11 @@
 
     CODE[...] = jnp.zeros_like(CODE)
     MASK[...] = jnp.zeros_like(MASK)
-    W1[...] = jnp.zeros_like(W1)
-    DN[pl.ds(dd_h.shape[1], LANES - dd_h.shape[1])] = jnp.zeros((LANES - dd_h.shape[1], width), BF16)
+    spare = LANES - dd_h.shape[1]
+    for ref, start in ((W1, LANES - spare), (W1, 2 * LANES - spare), (DN, LANES - spare)):
+        ref[pl.ds(start, spare)] = jnp.zeros((spare, width), BF16)
     for m in range(n_micro):
-        ids = routes[0, m]
+        ids = jnp.concatenate([routes[0, t, m : m + 1] for t in range(n_tok)], axis=0)
         lane = lax.broadcasted_iota(jnp.int32, (n_tok, LANES), 1)
         named = jnp.zeros((n_tok, LANES), F32)
         for k in range(topk):
@@ -106,10 +113,6 @@
     def rs_refs(m, p, s, o):
         axis = order[p][2 - s]
         there = lax.rem(me[axis] + o, sizes[axis])
-        if s == 0:
-            at = [slice(None)] * 3
-            at[axis] = there
-            return PT.at[m, at[0], at[1], at[2], :, pl.ds(offs[p], part)], R1.at[m, p, o - 1]
         if s == 1:
             rest = [d for d in range(3) if d != order[p][2]]
             at = [slice(None)] * 2
@@ -120,7 +123,7 @@
     def rs_copy(m, p, s, o):
         src, dst = rs_refs(m, p, s, o)
         return pltpu.make_async_remote_copy(
-            src_ref=src, dst_ref=dst, send_sem=rs_s.at[m, p, s, o - 1], recv_sem=rs_r.at[m, p, s, o - 1],
+            src_ref=src, dst_ref=dst, send_sem=rs_s.at[m, p, s - 1, o - 1], recv_sem=rs_r.at[m, p, s - 1, o - 1],
             device_id=peer(order[p][2 - s], o), device_id_type=MESH)
 
     def rs_start(m, p, s):
@@ -131,6 +134,62 @@
         for o in range(1, sizes[order[p][2 - s]]):
             rs_copy(m, p, s, o).wait_recv()
 
+    def plane(ref, m, axis, there, start, size):
+        at = [slice(None)] * 3
+        at[axis] = there
+        return ref.at[m, at[0], at[1], at[2], :, pl.ds(start, size)]
+
+    def far_gather(m, p, k):
+        axis = order[p][2]
+        right = k in (0, 2, 4)
+        low = k in (0, 3, 4)
+        owner = lax.rem(me[axis] + sizes[axis] + (-1 if k == 4 else 1 if k == 5 else 0), sizes[axis])
+        half = part // 2
+        ref = plane(G, m, axis, owner, offs[p] if low else offs[p] + half, half if low else gw[p] - half)
+        return pltpu.make_async_remote_copy(
+            src_ref=ref, dst_ref=ref, send_sem=fa_s.at[m, p, k], recv_sem=fa_r.at[m, p, k],
+            device_id=peer(axis, 1 if right else -1), device_id_type=MESH)
+
+    def far_reduce(m, p, k):
+        axis = order[p][2]
+        n = sizes[axis]
+        right = k in (0, 2, 4)
+        low = k in (0, 3, 4)
+        half = part // 2
+        there = lax.rem(me[axis] + (2 if k < 2 else 1 if right else n - 1), n)
+        src = plane(PT, m, axis, there, offs[p] + (0 if low else half), half)
+        side = 0 if right else 1
+        dst = RA.at[m, p, side] if k < 2 else RB.at[m, p, side, :, :, :, pl.ds(0 if low else half, half)]
+        return pltpu.make_async_remote_copy(
+            src_ref=src, dst_ref=dst, send_sem=fr_s.at[m, p, k], recv_sem=fr_r.at[m, p, k],
+            device_id=peer(axis, 1 if right else -1), device_id_type=MESH)
+
+    def forward(m):
+        for p in range(3):
+            for k in (0, 1):
+                far_gather(m, p, k).wait_recv()
+                far_gather(m, p, k + 4).start()
+
+    def merge(m):
+        half = part // 2
+        for p in range(3):
+            axis = order[p][2]
+            rest = [d for d in range(3) if d != axis]
+            for k in (0, 1):
+                far_reduce(m, p, k).wait_recv()
+                there = lax.rem(me[axis] + (1 if k == 0 else sizes[axis] - 1), sizes[axis])
+
+                def add(i, carry):
+                    at = [slice(None)] * 3
+                    at[axis] = there
+                    at[rest[0]] = i
+                    where = (m, at[0], at[1], at[2], slice(None), pl.ds(offs[p] + k * half, half))
+                    PT[where] = (PT[where].astype(F32) + RA[m, p, k, i].astype(F32)).astype(BF16)
+                    return carry
+
+                lax.fori_loop(0, sizes[rest[0]], add, 0)
+                far_reduce(m, p, k + 4).start()
+
     def tp_copy(m):
         return pltpu.make_async_remote_copy(
             src_ref=TS.at[m], dst_ref=TR.at[m], send_sem=tp_s.at[m], recv_sem=tp_r.at[m],
@@ -144,7 +203,8 @@
     def take_input(m):
         @pl.when(sec == 0)
         def _():
-            X[m, 0:n_tok] = acts[m]
+            for t in range(n_tok):
+                X[m, t : t + 1] = acts[t, m : m + 1]
 
         @pl.when(sec == 1)
         def _():
@@ -161,7 +221,7 @@
 
     def zero_share(m):
         normed = G[m, me[0], me[1], me[2], :, pl.ds(0, width)]
-        gates = jax.nn.sigmoid(jnp.dot(normed, RT[...], preferred_element_type=F32))
+        gates = jax.nn.sigmoid(dot_t(normed, RT[...]))
         lane = lax.broadcasted_iota(jnp.int32, gates.shape, 1)
         share = jnp.where(lane >= n_real, MASK[m][:, :n_total] * gates, 0.0)
         ZS[m] = jnp.broadcast_to(jnp.sum(share, axis=-1, keepdims=True), (ROWS, LANES))
@@ -172,7 +232,7 @@
     def compute(m):
         hid = jnp.zeros((rows, 2 * LANES), F32)
         for p in range(3):
-            hid += jnp.dot(tokens(m, offs[p], part), W1[pl.ds(offs[p], part)], preferred_element_type=F32)
+            hid += dot_t(tokens(m, offs[p], part), W1[:, pl.ds(offs[p], part)])
         LH[:, 0:LANES] = (jax.nn.silu(hid[:, :LANES]) * hid[:, LANES:]).astype(BF16)
         codes = tokens(m, width, LANES)
         pick = (lax.broadcasted_iota(jnp.int32, (LANES, n_slots), 0) == group).astype(BF16)
@@ -182,7 +242,7 @@
         hit = (tok // ROWS == slot // slots) & (col == (slot % slots + 1).astype(F32))
         LH[:, LANES:] = jnp.where(hit, 1.0, 0.0).astype(BF16)
         pick_t = (lax.broadcasted_iota(jnp.int32, (ROWS, LANES), 1) == group).astype(BF16)
-        row = lax.dot_general(pick_t, codes, (((1,), (1,)), ((), ())), preferred_element_type=F32)[0:1]
+        row = dot_t(pick_t, codes)[0:1]
         slot = lax.broadcasted_iota(jnp.int32, (n_slots, rows), 0)
         tok = lax.broadcasted_iota(jnp.int32, (n_slots, rows), 1)
         hit = (tok // ROWS == slot // slots) & (row == (slot % slots + 1).astype(F32))
@@ -190,7 +250,7 @@
         for c in range(0, width, chunk):
             CH[:, pl.ds(c, chunk)] = jnp.dot(chooser, tokens(m, c, chunk), preferred_element_type=F32).astype(BF16)
         chosen = CH[...]
-        logit = jnp.dot(chosen, RT[...], preferred_element_type=F32)
+        logit = dot_t(chosen, RT[...])
         lane = lax.broadcasted_iota(jnp.int32, logit.shape, 1)
         coef = jax.nn.sigmoid(jnp.sum(jnp.where(lane == group, logit, 0.0), axis=-1, keepdims=True))
         gate = jnp.dot(chosen, EG[...], preferred_element_type=F32)
@@ -203,7 +263,8 @@
             for c in range(offs[p], offs[p] + part, chunk):
                 both = jnp.dot(LH[...], DN[:, pl.ds(c, chunk)], preferred_element_type=F32).astype(BF16)
                 PT[m, :, :, :, :, pl.ds(c, chunk)] = both.reshape(*sizes, ROWS, chunk)
-            rs_start(m, p, 0)
+            for k in range(4):
+                far_reduce(m, p, k).start()
 
     def rs_sum(m, p, s):
         axis = order[p][2 - s]
@@ -216,8 +277,8 @@
                 at[axis] = me[axis]
                 at[rest[0]] = i
                 total = PT[m, at[0], at[1], at[2], :, pl.ds(offs[p], part)].astype(F32)
-                for o in range(n - 1):
-                    total += R1[m, p, o, i].astype(F32)
+                for side in range(2):
+                    total += RB[m, p, side, i].astype(F32)
                 S1[m, p, i] = total.astype(BF16)
                 return carry
 
@@ -242,43 +303,89 @@
         summed = TS[m].astype(F32) + TR[m].astype(F32)
         done = (X[m].astype(F32) + summed + ZS[m][:, 0:1] * normed).astype(BF16)
         OB[m] = done
-        out[0, m] = done[0:n_tok]
+        for t in range(n_tok):
+            out[0, t, m : m + 1] = done[t : t + 1]
 
         @pl.when(sec == 0)
         def _():
             pp_copy(m).start()
 
-    for m in range(n_micro):
+    def enter(m):
         take_input(m)
         norm_and_send(m)
-        if m == 0:
-            for c in weight_copies():
-                c.wait()
-            W1[:, 0 : DG.shape[1]] = DG[...]
-            W1[:, LANES : LANES + DU.shape[1]] = DU[...]
-        zero_share(m)
-        for s in range(3):
-            for p in range(3):
+
+    def gather(m, s):
+        for p in range(3):
+            if s < 2:
                 ag_wait(m, p, s)
-                if s < 2:
-                    ag_start(m, p, s + 1)
-        compute(m)
-        for s in range(3):
-            for p in range(3):
+            else:
+                for k in range(2, 6):
+                    far_gather(m, p, k).wait_recv()
+            if s == 0:
+                ag_start(m, p, 1)
+            elif s == 1:
+                for k in range(4):
+                    far_gather(m, p, k).start()
+
+    def reduce(m, s):
+        for p in range(3):
+            if s == 0:
+                for k in range(2, 6):
+                    far_reduce(m, p, k).wait_recv()
+            else:
                 rs_wait(m, p, s)
-                rs_sum(m, p, s)
-                if s < 2:
-                    rs_start(m, p, s + 1)
-        tp_copy(m).start()
-        finish(m)
+            rs_sum(m, p, s)
+            if s < 2:
+                rs_start(m, p, s + 1)
+        if s == 2:
+            tp_copy(m).start()
+
+    def only(section, *steps):
+        @pl.when(sec == section)
+        def _():
+            for step in steps:
+                step()
+
+    enter(0)
+    only(0, lambda: enter(1))
+    gather(0, 0)
+    gather(0, 1)
+    only(0, lambda: gather(1, 0))
+    forward(0)
+    only(0, lambda: gather(1, 1))
+    for c in weight_copies():
+        c.wait()
+    zero_share(0)
+    gather(0, 2)
+    compute(0)
+    only(0, lambda: forward(1))
+    merge(0)
+    reduce(0, 0)
+    only(1, lambda: enter(1))
+    reduce(0, 1)
+    only(1, lambda: gather(1, 0))
+    reduce(0, 2)
+    only(1, lambda: gather(1, 1))
+    finish(0)
+    only(1, lambda: forward(1))
+    zero_share(1)
+    gather(1, 2)
+    compute(1)
+    merge(1)
+    for s in range(3):
+        reduce(1, s)
+    finish(1)
 
     for m in range(n_micro):
         for p in range(3):
-            for s in range(3):
+            for s in range(2):
                 for o in range(1, sizes[order[p][s]]):
                     ag_copy(m, p, s, o).wait_send()
-                for o in range(1, sizes[order[p][2 - s]]):
-                    rs_copy(m, p, s, o).wait_send()
+                for o in range(1, sizes[order[p][1 - s]]):
+                    rs_copy(m, p, s + 1, o).wait_send()
+            for k in range(6):
+                far_gather(m, p, k).wait_send()
+                far_reduce(m, p, k).wait_send()
         tp_copy(m).wait_send()
 
         @pl.when(sec == 0)
@@ -287,9 +394,14 @@
 
 
 def on_device(sizes, n_tp, acts, routes, gain, router, dg, du, dd, eg, eu, ed):
-    n_micro, n_tok, width = acts.shape
+    swapped = (jnp.swapaxes(acts, 0, 1), jnp.swapaxes(routes, 1, 2), gain, *(jnp.swapaxes(w, 1, 2) for w in (router, dg, du)))
+    return jnp.swapaxes(in_vmem(sizes, n_tp, *swapped, dd, eg, eu, ed), 1, 2)
+
+
+def in_vmem(sizes, n_tp, acts, routes, gain, router, dg, du, dd, eg, eu, ed):
+    n_tok, n_micro, width = acts.shape
     topk = routes.shape[-1]
-    n_total = router.shape[-1]
+    n_total = router.shape[1]
     n_blocks = sizes[0] * sizes[1] * sizes[2]
     slots = max(2, (n_tok * topk + n_total - 1) // n_total)
     n_slots = n_blocks * slots
@@ -302,7 +414,8 @@
     scratch = [
         vm((n_micro, *sizes, ROWS, width + LANES), BF16),
         vm((n_micro, *sizes, ROWS, width), BF16),
-        vm((n_micro, 3, n - 1, n, n, ROWS, part), BF16),
+        vm((n_micro, 3, 2, n, n, ROWS, part // 2), BF16),
+        vm((n_micro, 3, 2, n, n, ROWS, part), BF16),
         vm((n_micro, 3, n, n, ROWS, part), BF16),
         vm((n_micro, 3, n - 1, n, ROWS, part), BF16),
         vm((n_micro, 3, n, ROWS, part), BF16),
@@ -314,33 +427,35 @@
         vm((n_micro, ROWS, LANES), F32),
         vm((n_micro, ROWS, LANES), F32),
         vm((n_micro, ROWS, LANES), F32),
-        vm((width, n_total), BF16),
-        vm((width, dg.shape[-1]), BF16),
-        vm((width, du.shape[-1]), BF16),
+        vm((n_total, width), BF16),
         vm((width, inner), BF16),
         vm((width, inner), BF16),
         vm((inner, width), BF16),
-        vm((width, 2 * LANES), BF16),
+        vm((2 * LANES, width), BF16),
         vm((n_blocks * ROWS, LANES + n_slots), BF16),
         vm((LANES + n_slots, width), BF16),
         vm((n_slots, width), BF16),
         pltpu.SemaphoreType.DMA((7,)),
-        pltpu.SemaphoreType.DMA((n_micro, 3, 3, n - 1)),
-        pltpu.SemaphoreType.DMA((n_micro, 3, 3, n - 1)),
-        pltpu.SemaphoreType.DMA((n_micro, 3, 3, n - 1)),
-        pltpu.SemaphoreType.DMA((n_micro, 3, 3, n - 1)),
+        pltpu.SemaphoreType.DMA((n_micro, 3, 2, n - 1)),
+        pltpu.SemaphoreType.DMA((n_micro, 3, 2, n - 1)),
+        pltpu.SemaphoreType.DMA((n_micro, 3, 2, n - 1)),
+        pltpu.SemaphoreType.DMA((n_micro, 3, 2, n - 1)),
+        pltpu.SemaphoreType.DMA((n_micro, 3, 6)),
+        pltpu.SemaphoreType.DMA((n_micro, 3, 6)),
+        pltpu.SemaphoreType.DMA((n_micro, 3, 6)),
+        pltpu.SemaphoreType.DMA((n_micro, 3, 6)),
         pltpu.SemaphoreType.DMA((n_micro,)),
         pltpu.SemaphoreType.DMA((n_micro,)),
         pltpu.SemaphoreType.DMA((n_micro,)),
         pltpu.SemaphoreType.DMA((n_micro,)),
     ]
-    in_vmem = pl.BlockSpec(memory_space=pltpu.VMEM)
+    held = pl.BlockSpec(memory_space=pltpu.VMEM)
     left = pl.BlockSpec(memory_space=pl.ANY)
     return pl.pallas_call(
         functools.partial(kernel, cfg),
-        out_shape=jax.ShapeDtypeStruct((1, n_micro, n_tok, width), BF16),
-        in_specs=[in_vmem] * 3 + [left] * 7,
-        out_specs=in_vmem,
+        out_shape=jax.ShapeDtypeStruct((1, n_tok, n_micro, width), BF16),
+        in_specs=[held] * 3 + [left] * 7,
+        out_specs=held,
         scratch_shapes=scratch,
         compiler_params=pltpu.CompilerParams(
             collective_id=0, has_side_effects=True, vmem_limit_bytes=60 * 1024 * 1024

time: 195 us -> 135 us (0.69)
  Pallas kernels: 183 us -> 133 us
  local copies, waits for them, and re-layouts: 10.9 us -> 1.57 us
    pallas_call x1, Pallas kernels: 183 us -> 133 us  [in_vmem(): pl.pallas_call(functools.partial(kernel, cfg), out_shape=jax.ShapeDtypeSt...]
    unnamed x5 -> x1, local copies, waits for them, and re-layouts: 9.32 us -> 1.57 us
where the time goes in v2:
time: 135 us
  Pallas kernels  133 us (99%)
  local copies, waits for them, and re-layouts  1.57 us (1%)
    pallas_call x1, Pallas kernels, in_vmem(): pl.pallas_call(functools.partial(kernel, cfg), out_shape=jax.ShapeDtypeSt...  133 us

profile of v2, /device:TPU:1, one launch (start us, length us, event | category | flops | bytes accessed | tf_op | source)
XLA Modules:
  0.0 134.9 jit_solution(16041587140978544953)
XLA Ops:
  0.0 133.4 %relay.1 = bf16[1,6,2,3072]{3,2,1,0:T(2,128)(2,1)} custom-call(bf16[6,2,3072]{2,1,0:T(2,128)(2,1)} %bitcast.10, s32[1,6,2,8]{3,2,1,0:T(2,128)} %bitcast.11, bf16[1,3072]{1,0:T(2,128)(2,1)} %refs_2_.1, bf16[1,96,3072]{2,1,0:T(8,128)(2,1)} %bitcast.6, bf16[1,48,3072]{2,1,0:T(8,128)(2,1)} %bitcast.8, bf16[1,48,3072]{2,1,0:T(8,128)(2,1)} %bitcast.9, ...), custom_call_target="tpu_custom_call" | custom-call | tf_op jit(solution)/shard_map/relay/pallas_call | solution.py:454
  133.4 1.6 %copy.12 = bf16[1,2,6,3072]{3,1,2,0:T(2,128)(2,1)} copy(bf16[1,2,6,3072]{3,1,2,0:T(2,128)(2,1)} %bitcast.7) | data formatting | bytes 147456

commit v3 on v2

--- a/solution.py
+++ b/solution.py
@@ -68,9 +68,8 @@
         for o in range(1, sizes[axis]):
             pl.semaphore_signal(barrier, inc=1, device_id=peer(axis, -o), device_id_type=MESH)
             greeted += 1
-    for who in (far, above):
-        pl.semaphore_signal(barrier, inc=1, device_id=who, device_id_type=MESH)
-        greeted += 1
+    pl.semaphore_signal(barrier, inc=1, device_id=above, device_id_type=MESH)
+    greeted += 1
 
     CODE[...] = jnp.zeros_like(CODE)
     MASK[...] = jnp.zeros_like(MASK)
@@ -139,60 +138,71 @@
         at[axis] = there
         return ref.at[m, at[0], at[1], at[2], :, pl.ds(start, size)]
 
-    def far_gather(m, p, k):
+    half, quarter = part // 2, part // 4
+
+    def lanes_of(p, way, k, width_p):
+        if k == 2:
+            return ((1 - way) * half, half if way == 1 else width_p - half)
+        start = way * half + (k % 3) * quarter
+        return (start, width_p - start if way == 1 and k % 3 == 1 else quarter)
+
+    def far_gather(m, p, way, k):
         axis = order[p][2]
-        right = k in (0, 2, 4)
-        low = k in (0, 3, 4)
-        owner = lax.rem(me[axis] + sizes[axis] + (-1 if k == 4 else 1 if k == 5 else 0), sizes[axis])
-        half = part // 2
-        ref = plane(G, m, axis, owner, offs[p] if low else offs[p] + half, half if low else gw[p] - half)
+        shift = 0 if k < 3 else (-1, 1)[way]
+        start, size = lanes_of(p, way, k, gw[p])
+        ref = plane(G, m, axis, lax.rem(me[axis] + sizes[axis] + shift, sizes[axis]), offs[p] + start, size)
         return pltpu.make_async_remote_copy(
-            src_ref=ref, dst_ref=ref, send_sem=fa_s.at[m, p, k], recv_sem=fa_r.at[m, p, k],
-            device_id=peer(axis, 1 if right else -1), device_id_type=MESH)
-
-    def far_reduce(m, p, k):
+            src_ref=ref, dst_ref=ref, send_sem=fa_s.at[m, p, way, k], recv_sem=fa_r.at[m, p, way, k],
+            device_id=peer(axis, (1, -1)[way]), device_id_type=MESH)
+
+    def far_reduce(m, p, way, k):
         axis = order[p][2]
         n = sizes[axis]
-        right = k in (0, 2, 4)
-        low = k in (0, 3, 4)
-        half = part // 2
-        there = lax.rem(me[axis] + (2 if k < 2 else 1 if right else n - 1), n)
-        src = plane(PT, m, axis, there, offs[p] + (0 if low else half), half)
-        side = 0 if right else 1
-        dst = RA.at[m, p, side] if k < 2 else RB.at[m, p, side, :, :, :, pl.ds(0 if low else half, half)]
+        start, size = lanes_of(p, way, k, part)
+        src = plane(PT, m, axis, lax.rem(me[axis] + (2 if k < 2 else (1, n - 1)[way]), n), offs[p] + start, size)
+        if k < 2:
+            dst = RA.at[m, p, way, :, :, :, pl.ds(k * quarter, quarter)]
+        else:
+            dst = RB.at[m, p, way, :, :, :, pl.ds(start, size)]
         return pltpu.make_async_remote_copy(
-            src_ref=src, dst_ref=dst, send_sem=fr_s.at[m, p, k], recv_sem=fr_r.at[m, p, k],
-            device_id=peer(axis, 1 if right else -1), device_id_type=MESH)
+            src_ref=src, dst_ref=dst, send_sem=fr_s.at[m, p, way, k], recv_sem=fr_r.at[m, p, way, k],
+            device_id=peer(axis, (1, -1)[way]), device_id_type=MESH)
+
+    def far_start(copy, m, p):
+        for k in range(3):
+            for way in range(2):
+                copy(m, p, way, k).start()
+
+    def far_wait(copy, m, p):
+        for k in range(2, 5):
+            for way in range(2):
+                copy(m, p, way, k).wait_recv()
 
     def forward(m):
-        for p in range(3):
-            for k in (0, 1):
-                far_gather(m, p, k).wait_recv()
-                far_gather(m, p, k + 4).start()
+        for k in range(2):
+            for p in range(3):
+                for way in range(2):
+                    far_gather(m, p, way, k).wait_recv()
+                    far_gather(m, p, way, k + 3).start()
 
     def merge(m):
-        half = part // 2
-        for p in range(3):
-            axis = order[p][2]
-            rest = [d for d in range(3) if d != axis]
-            for k in (0, 1):
-                far_reduce(m, p, k).wait_recv()
-                there = lax.rem(me[axis] + (1 if k == 0 else sizes[axis] - 1), sizes[axis])
-
-                def add(i, carry):
+        for k in range(2):
+            for p in range(3):
+                axis = order[p][2]
+                rest = [d for d in range(3) if d != axis]
+                for way in range(2):
+                    far_reduce(m, p, way, k).wait_recv()
                     at = [slice(None)] * 3
-                    at[axis] = there
-                    at[rest[0]] = i
-                    where = (m, at[0], at[1], at[2], slice(None), pl.ds(offs[p] + k * half, half))
-                    PT[where] = (PT[where].astype(F32) + RA[m, p, k, i].astype(F32)).astype(BF16)
-                    return carry
-
-                lax.fori_loop(0, sizes[rest[0]], add, 0)
-                far_reduce(m, p, k + 4).start()
-
-    def tp_copy(m):
+                    at[axis] = lax.rem(me[axis] + (1, sizes[axis] - 1)[way], sizes[axis])
+                    where = (m, *at, slice(None), pl.ds(offs[p] + way * half + k * quarter, quarter))
+                    come = RA[m, p, way, :, :, :, pl.ds(k * quarter, quarter)].astype(F32)
+                    PT[where] = (PT[where].astype(F32) + come).astype(BF16)
+                    far_reduce(m, p, way, k + 3).start()
+
+    def tp_copy(m, p):
+        lanes = pl.ds(offs[p], part)
         return pltpu.make_async_remote_copy(
-            src_ref=TS.at[m], dst_ref=TR.at[m], send_sem=tp_s.at[m], recv_sem=tp_r.at[m],
+            src_ref=TS.at[m, :, lanes], dst_ref=TR.at[m, :, lanes], send_sem=tp_s.at[m, p], recv_sem=tp_r.at[m, p],
             device_id=far, device_id_type=MESH)
 
     def pp_copy(m):
@@ -229,7 +239,7 @@
     def tokens(m, start, size):
         return G[m, :, :, :, :, pl.ds(start, size)].reshape(rows, size)
 
-    def compute(m):
+    def work(m):
         hid = jnp.zeros((rows, 2 * LANES), F32)
         for p in range(3):
             hid += dot_t(tokens(m, offs[p], part), W1[:, pl.ds(offs[p], part)])
@@ -259,12 +269,13 @@
         for c in range(0, width, chunk):
             made = jnp.dot(inner, ED[:, pl.ds(c, chunk)], preferred_element_type=F32)
             DN[pl.ds(LANES, n_slots), pl.ds(c, chunk)] = (coef * made).astype(BF16)
+
+    def put_out(m):
         for p in range(3):
             for c in range(offs[p], offs[p] + part, chunk):
                 both = jnp.dot(LH[...], DN[:, pl.ds(c, chunk)], preferred_element_type=F32).astype(BF16)
                 PT[m, :, :, :, :, pl.ds(c, chunk)] = both.reshape(*sizes, ROWS, chunk)
-            for k in range(4):
-                far_reduce(m, p, k).start()
+            far_start(far_reduce, m, p)
 
     def rs_sum(m, p, s):
         axis = order[p][2 - s]
@@ -298,7 +309,8 @@
             TS[m, :, pl.ds(offs[p], part)] = total.astype(BF16)
 
     def finish(m):
-        tp_copy(m).wait_recv()
+        for p in range(3):
+            tp_copy(m, p).wait_recv()
         normed = G[m, me[0], me[1], me[2], :, pl.ds(0, width)].astype(F32)
         summed = TS[m].astype(F32) + TR[m].astype(F32)
         done = (X[m].astype(F32) + summed + ZS[m][:, 0:1] * normed).astype(BF16)
@@ -319,26 +331,23 @@
             if s < 2:
                 ag_wait(m, p, s)
             else:
-                for k in range(2, 6):
-                    far_gather(m, p, k).wait_recv()
+                far_wait(far_gather, m, p)
             if s == 0:
                 ag_start(m, p, 1)
             elif s == 1:
-                for k in range(4):
-                    far_gather(m, p, k).start()
+                far_start(far_gather, m, p)
 
     def reduce(m, s):
         for p in range(3):
             if s == 0:
-                for k in range(2, 6):
-                    far_reduce(m, p, k).wait_recv()
+                far_wait(far_reduce, m, p)
             else:
                 rs_wait(m, p, s)
             rs_sum(m, p, s)
             if s < 2:
                 rs_start(m, p, s + 1)
-        if s == 2:
-            tp_copy(m).start()
+            else:
+                tp_copy(m, p).start()
 
     def only(section, *steps):
         @pl.when(sec == section)
@@ -349,31 +358,31 @@
     enter(0)
     only(0, lambda: enter(1))
     gather(0, 0)
+    only(1, lambda: enter(1))
+    gather(1, 0)
     gather(0, 1)
-    only(0, lambda: gather(1, 0))
     forward(0)
-    only(0, lambda: gather(1, 1))
+    gather(1, 1)
     for c in weight_copies():
         c.wait()
     zero_share(0)
     gather(0, 2)
-    compute(0)
-    only(0, lambda: forward(1))
-    merge(0)
-    reduce(0, 0)
-    only(1, lambda: enter(1))
-    reduce(0, 1)
-    only(1, lambda: gather(1, 0))
-    reduce(0, 2)
-    only(1, lambda: gather(1, 1))
-    finish(0)
-    only(1, lambda: forward(1))
+    forward(1)
+    work(0)
+    put_out(0)
     zero_share(1)
     gather(1, 2)
-    compute(1)
+    work(1)
+    merge(0)
+    put_out(1)
     merge(1)
-    for s in range(3):
-        reduce(1, s)
+    reduce(0, 0)
+    reduce(1, 0)
+    reduce(0, 1)
+    reduce(1, 1)
+    reduce(0, 2)
+    reduce(1, 2)
+    finish(0)
     finish(1)
 
     for m in range(n_micro):
@@ -383,11 +392,11 @@
                     ag_copy(m, p, s, o).wait_send()
                 for o in range(1, sizes[order[p][1 - s]]):
                     rs_copy(m, p, s + 1, o).wait_send()
-            for k in range(6):
-                far_gather(m, p, k).wait_send()
-                far_reduce(m, p, k).wait_send()
-        tp_copy(m).wait_send()
-
+            for k in range(5):
+                for way in range(2):
+                    far_gather(m, p, way, k).wait_send()
+                    far_reduce(m, p, way, k).wait_send()
+            tp_copy(m, p).wait_send()
         @pl.when(sec == 0)
         def _():
             pp_copy(m).wait_send()
@@ -440,17 +449,17 @@
         pltpu.SemaphoreType.DMA((n_micro, 3, 2, n - 1)),
         pltpu.SemaphoreType.DMA((n_micro, 3, 2, n - 1)),
         pltpu.SemaphoreType.DMA((n_micro, 3, 2, n - 1)),
-        pltpu.SemaphoreType.DMA((n_micro, 3, 6)),
-        pltpu.SemaphoreType.DMA((n_micro, 3, 6)),
-        pltpu.SemaphoreType.DMA((n_micro, 3, 6)),
-        pltpu.SemaphoreType.DMA((n_micro, 3, 6)),
-        pltpu.SemaphoreType.DMA((n_micro,)),
-        pltpu.SemaphoreType.DMA((n_micro,)),
+        pltpu.SemaphoreType.DMA((n_micro, 3, 2, 5)),
+        pltpu.SemaphoreType.DMA((n_micro, 3, 2, 5)),
+        pltpu.SemaphoreType.DMA((n_micro, 3, 2, 5)),
+        pltpu.SemaphoreType.DMA((n_micro, 3, 2, 5)),
+        pltpu.SemaphoreType.DMA((n_micro, 3)),
+        pltpu.SemaphoreType.DMA((n_micro, 3)),
         pltpu.SemaphoreType.DMA((n_micro,)),
         pltpu.SemaphoreType.DMA((n_micro,)),
     ]
     held = pl.BlockSpec(memory_space=pltpu.VMEM)
-    left = pl.BlockSpec(memory_space=pl.ANY)
+    left = pl.BlockSpec(memory_space=pltpu.HBM)
     return pl.pallas_call(
         functools.partial(kernel, cfg),
         out_shape=jax.ShapeDtypeStruct((1, n_tok, n_micro, width), BF16),

time: 135 us -> 114 us (0.84)
  Pallas kernels: 133 us -> 113 us
    pallas_call x1, Pallas kernels: 133 us -> 113 us  [in_vmem(): pl.pallas_call(functools.partial(kernel, cfg), out_shape=jax.ShapeDtypeSt...]
where the time goes in v3:
time: 114 us
  Pallas kernels  113 us (99%)
  local copies, waits for them, and re-layouts  1.57 us (1%)
    pallas_call x1, Pallas kernels, in_vmem(): pl.pallas_call(functools.partial(kernel, cfg), out_shape=jax.ShapeDtypeSt...  113 us

profile of v3, /device:TPU:1, one launch (start us, length us, event | category | flops | bytes accessed | tf_op | source)
XLA Modules:
  0.0 114.1 jit_solution(3585077420956393095)
XLA Ops:
  0.0 112.5 %relay.1 = bf16[1,6,2,3072]{3,2,1,0:T(2,128)(2,1)} custom-call(bf16[6,2,3072]{2,1,0:T(2,128)(2,1)} %bitcast.10, s32[1,6,2,8]{3,2,1,0:T(2,128)} %bitcast.11, bf16[1,3072]{1,0:T(2,128)(2,1)} %refs_2_.1, bf16[1,96,3072]{2,1,0:T(8,128)(2,1)} %bitcast.6, bf16[1,48,3072]{2,1,0:T(8,128)(2,1)} %bitcast.8, bf16[1,48,3072]{2,1,0:T(8,128)(2,1)} %bitcast.9, ...), custom_call_target="tpu_custom_call" | custom-call | tf_op jit(solution)/shard_map/relay/pallas_call | solution.py:463
  112.5 1.6 %copy.12 = bf16[1,2,6,3072]{3,1,2,0:T(2,128)(2,1)} copy(bf16[1,2,6,3072]{3,1,2,0:T(2,128)(2,1)} %bitcast.7) | data formatting | bytes 147456

commit v4 on v3

--- a/solution.py
+++ b/solution.py
@@ -17,15 +17,19 @@
 LANES = 128
 
 
+def farthest_first(n):
+    return sorted(range(1, n), key=lambda o: -min(o, n - o))
+
+
 def dot_t(a, b):
     return lax.dot_general(a, b, (((1,), (1,)), ((), ())), preferred_element_type=F32)
 
 
 def kernel(cfg, *refs):
     (acts, routes, gain, router_h, dg_h, du_h, dd_h, eg_h, eu_h, ed_h, out) = refs[:11]
-    (G, PT, RA, RB, S1, R2, S2, R3, TS, TR, X, OB, CODE, MASK, ZS) = refs[11:26]
-    (RT, EG, EU, ED, W1, LH, DN, CH) = refs[26:34]
-    (w_sem, ag_s, ag_r, rs_s, rs_r, fa_s, fa_r, fr_s, fr_r, tp_s, tp_r, pp_s, pp_r) = refs[34:]
+    (G, PT, RA, RB, S1, R2, S2, R3, TS, TR, TL, BASE, BL, X, OB, CODE, MASK) = refs[11:28]
+    (RT, EG, EU, ED, W1, LH, DN, CH) = refs[28:36]
+    (w_sem, ag_s, ag_r, rs_s, rs_r, fa_s, fa_r, fr_s, fr_r, tp_s, tp_r, tl_s, tl_r, pp_s, pp_r) = refs[36:]
     sizes, n_tp, width, n_micro, n_tok, topk, n_real, n_total, slots, chunk = cfg
     n_blocks = sizes[0] * sizes[1] * sizes[2]
     rows = n_blocks * ROWS
@@ -48,7 +52,7 @@
         z = lax.rem(tp * n + me[1] + step + n * n_tp, n * n_tp)
         return {"ep_1": lax.rem(z, n), "tp": z // n}
 
-    far = {"tp": 1 - tp}
+    far_last = {"tp": 1 - tp, "pp": 1}
     above = {"pp": 1 - sec}
 
     def weight_copies():
@@ -102,7 +106,7 @@
             device_id=peer(axes[s], o), device_id_type=MESH)
 
     def ag_start(m, p, s):
-        for o in range(1, sizes[order[p][s]]):
+        for o in farthest_first(sizes[order[p][s]]):
             ag_copy(m, p, s, o).start()
 
     def ag_wait(m, p, s):
@@ -126,7 +130,7 @@
             device_id=peer(order[p][2 - s], o), device_id_type=MESH)
 
     def rs_start(m, p, s):
-        for o in range(1, sizes[order[p][2 - s]]):
+        for o in farthest_first(sizes[order[p][2 - s]]):
             rs_copy(m, p, s, o).start()
 
     def rs_wait(m, p, s):
@@ -199,15 +203,26 @@
                     PT[where] = (PT[where].astype(F32) + come).astype(BF16)
                     far_reduce(m, p, way, k + 3).start()
 
-    def tp_copy(m, p):
+    def tp_copy(m, p, section):
         lanes = pl.ds(offs[p], part)
         return pltpu.make_async_remote_copy(
-            src_ref=TS.at[m, :, lanes], dst_ref=TR.at[m, :, lanes], send_sem=tp_s.at[m, p], recv_sem=tp_r.at[m, p],
-            device_id=far, device_id_type=MESH)
-
-    def pp_copy(m):
-        return pltpu.make_async_remote_copy(
-            src_ref=OB.at[m], dst_ref=X.at[m], send_sem=pp_s.at[m], recv_sem=pp_r.at[m],
+            src_ref=TS.at[m, :, lanes], dst_ref=TR.at[section, m, :, lanes], send_sem=tp_s.at[m, p],
+            recv_sem=tp_r.at[section, m, p], device_id=far_last, device_id_type=MESH)
+
+    def own_copy(m, p):
+        lanes = pl.ds(offs[p], part)
+        return pltpu.make_async_remote_copy(
+            src_ref=TS.at[m, :, lanes], dst_ref=TL.at[m, :, lanes], send_sem=tl_s.at[m, p], recv_sem=tl_r.at[m, p],
+            device_id=above, device_id_type=MESH)
+
+    def base_copy(m):
+        return pltpu.make_async_remote_copy(
+            src_ref=BASE.at[m], dst_ref=BL.at[m], send_sem=pp_s.at[0, m], recv_sem=pp_r.at[0, m],
+            device_id=above, device_id_type=MESH)
+
+    def back_copy(m):
+        return pltpu.make_async_remote_copy(
+            src_ref=X.at[m], dst_ref=OB.at[m], send_sem=pp_s.at[1, m], recv_sem=pp_r.at[1, m],
             device_id=above, device_id_type=MESH)
 
     def take_input(m):
@@ -218,7 +233,12 @@
 
         @pl.when(sec == 1)
         def _():
-            pp_copy(m).wait_recv()
+            base_copy(m).wait_recv()
+            for p in range(3):
+                own_copy(m, p).wait_recv()
+                tp_copy(m, p, 0).wait_recv()
+            X[m] = (BL[m] + (TL[m].astype(F32) + TR[0, m].astype(F32))).astype(BF16)
+            back_copy(m).start()
 
     def norm_and_send(m):
         wide = X[m].astype(F32)
@@ -234,16 +254,22 @@
         gates = jax.nn.sigmoid(dot_t(normed, RT[...]))
         lane = lax.broadcasted_iota(jnp.int32, gates.shape, 1)
         share = jnp.where(lane >= n_real, MASK[m][:, :n_total] * gates, 0.0)
-        ZS[m] = jnp.broadcast_to(jnp.sum(share, axis=-1, keepdims=True), (ROWS, LANES))
+        share = jnp.sum(share, axis=-1, keepdims=True)
+        BASE[m] = X[m].astype(F32) + share * normed.astype(F32)
+
+        @pl.when(sec == 0)
+        def _():
+            base_copy(m).start()
 
     def tokens(m, start, size):
         return G[m, :, :, :, :, pl.ds(start, size)].reshape(rows, size)
 
     def work(m):
-        hid = jnp.zeros((rows, 2 * LANES), F32)
-        for p in range(3):
-            hid += dot_t(tokens(m, offs[p], part), W1[:, pl.ds(offs[p], part)])
-        LH[:, 0:LANES] = (jax.nn.silu(hid[:, :LANES]) * hid[:, LANES:]).astype(BF16)
+        mid = rows // 2
+        for h in range(2):
+            some = G[m, h * (sizes[0] // 2) : (h + 1) * (sizes[0] // 2), :, :, :, pl.ds(0, width)].reshape(mid, width)
+            hid = dot_t(some, W1[...])
+            LH[h * mid : (h + 1) * mid, 0:LANES] = (jax.nn.silu(hid[:, :LANES]) * hid[:, LANES:]).astype(BF16)
         codes = tokens(m, width, LANES)
         pick = (lax.broadcasted_iota(jnp.int32, (LANES, n_slots), 0) == group).astype(BF16)
         col = jnp.dot(codes, pick, preferred_element_type=F32)
@@ -257,6 +283,8 @@
         tok = lax.broadcasted_iota(jnp.int32, (n_slots, rows), 1)
         hit = (tok // ROWS == slot // slots) & (row == (slot % slots + 1).astype(F32))
         chooser = jnp.where(hit, 1.0, 0.0).astype(BF16)
+        if m == 0:
+            forward(1)
         for c in range(0, width, chunk):
             CH[:, pl.ds(c, chunk)] = jnp.dot(chooser, tokens(m, c, chunk), preferred_element_type=F32).astype(BF16)
         chosen = CH[...]
@@ -309,18 +337,19 @@
             TS[m, :, pl.ds(offs[p], part)] = total.astype(BF16)
 
     def finish(m):
-        for p in range(3):
-            tp_copy(m, p).wait_recv()
-        normed = G[m, me[0], me[1], me[2], :, pl.ds(0, width)].astype(F32)
-        summed = TS[m].astype(F32) + TR[m].astype(F32)
-        done = (X[m].astype(F32) + summed + ZS[m][:, 0:1] * normed).astype(BF16)
-        OB[m] = done
-        for t in range(n_tok):
-            out[0, t, m : m + 1] = done[t : t + 1]
-
         @pl.when(sec == 0)
         def _():
-            pp_copy(m).start()
+            back_copy(m).wait_recv()
+            for t in range(n_tok):
+                out[0, t, m : m + 1] = OB[m, t : t + 1]
+
+        @pl.when(sec == 1)
+        def _():
+            for p in range(3):
+                tp_copy(m, p, 1).wait_recv()
+            done = (BASE[m] + (TS[m].astype(F32) + TR[1, m].astype(F32))).astype(BF16)
+            for t in range(n_tok):
+                out[0, t, m : m + 1] = done[t : t + 1]
 
     def enter(m):
         take_input(m)
@@ -347,7 +376,11 @@
             if s < 2:
                 rs_start(m, p, s + 1)
             else:
-                tp_copy(m, p).start()
+                tp_copy(m, p, sec).start()
+
+                @pl.when(sec == 0)
+                def _():
+                    own_copy(m, p).start()
 
     def only(section, *steps):
         @pl.when(sec == section)
@@ -366,11 +399,10 @@
     for c in weight_copies():
         c.wait()
     zero_share(0)
+    zero_share(1)
     gather(0, 2)
-    forward(1)
     work(0)
     put_out(0)
-    zero_share(1)
     gather(1, 2)
     work(1)
     merge(0)
@@ -396,10 +428,17 @@
                 for way in range(2):
                     far_gather(m, p, way, k).wait_send()
                     far_reduce(m, p, way, k).wait_send()
-            tp_copy(m, p).wait_send()
+            tp_copy(m, p, sec).wait_send()
+
         @pl.when(sec == 0)
         def _():
-            pp_copy(m).wait_send()
+            for p in range(3):
+                own_copy(m, p).wait_send()
+            base_copy(m).wait_send()
+
+        @pl.when(sec == 1)
+        def _():
+            back_copy(m).wait_send()
 
 
 def on_device(sizes, n_tp, acts, routes, gain, router, dg, du, dd, eg, eu, ed):
@@ -430,10 +469,12 @@
         vm((n_micro, 3, n, ROWS, part), BF16),
         vm((n_micro, 3, n - 1, ROWS, part), BF16),
         vm((n_micro, ROWS, width), BF16),
+        vm((2, n_micro, ROWS, width), BF16),
+        vm((n_micro, ROWS, width), BF16),
+        vm((n_micro, ROWS, width), F32),
+        vm((n_micro, ROWS, width), F32),
         vm((n_micro, ROWS, width), BF16),
         vm((n_micro, ROWS, width), BF16),
-        vm((n_micro, ROWS, width), BF16),
-        vm((n_micro, ROWS, LANES), F32),
         vm((n_micro, ROWS, LANES), F32),
         vm((n_micro, ROWS, LANES), F32),
         vm((n_total, width), BF16),
@@ -454,9 +495,11 @@
         pltpu.SemaphoreType.DMA((n_micro, 3, 2, 5)),
         pltpu.SemaphoreType.DMA((n_micro, 3, 2, 5)),
         pltpu.SemaphoreType.DMA((n_micro, 3)),
+        pltpu.SemaphoreType.DMA((2, n_micro, 3)),
         pltpu.SemaphoreType.DMA((n_micro, 3)),
-        pltpu.SemaphoreType.DMA((n_micro,)),
-        pltpu.SemaphoreType.DMA((n_micro,)),
+        pltpu.SemaphoreType.DMA((n_micro, 3)),
+        pltpu.SemaphoreType.DMA((2, n_micro)),
+        pltpu.SemaphoreType.DMA((2, n_micro)),
     ]
     held = pl.BlockSpec(memory_space=pltpu.VMEM)
     left = pl.BlockSpec(memory_space=pltpu.HBM)

time: 114 us -> 111 us (0.974)
  Pallas kernels: 113 us -> 109 us
    pallas_call x1, Pallas kernels: 113 us -> 109 us  [in_vmem(): pl.pallas_call(functools.partial(kernel, cfg), out_shape=jax.ShapeDtypeSt...]
where the time goes in v4:
time: 111 us
  Pallas kernels  109 us (98%)
  local copies, waits for them, and re-layouts  1.57 us (1%)
    pallas_call x1, Pallas kernels, in_vmem(): pl.pallas_call(functools.partial(kernel, cfg), out_shape=jax.ShapeDtypeSt...  109 us

profile of v4, /device:TPU:1, one launch (start us, length us, event | category | flops | bytes accessed | tf_op | source)
XLA Modules:
  0.0 110.9 jit_solution(10708138011748138031)
XLA Ops:
  0.0 109.3 %relay.1 = bf16[1,6,2,3072]{3,2,1,0:T(2,128)(2,1)} custom-call(bf16[6,2,3072]{2,1,0:T(2,128)(2,1)} %bitcast.10, s32[1,6,2,8]{3,2,1,0:T(2,128)} %bitcast.11, bf16[1,3072]{1,0:T(2,128)(2,1)} %refs_2_.1, bf16[1,96,3072]{2,1,0:T(8,128)(2,1)} %bitcast.6, bf16[1,48,3072]{2,1,0:T(8,128)(2,1)} %bitcast.8, bf16[1,48,3072]{2,1,0:T(8,128)(2,1)} %bitcast.9, ...), custom_call_target="tpu_custom_call" | custom-call | tf_op jit(solution)/shard_map/relay/pallas_call | solution.py:506
  109.3 1.6 %copy.12 = bf16[1,2,6,3072]{3,1,2,0:T(2,128)(2,1)} copy(bf16[1,2,6,3072]{3,1,2,0:T(2,128)(2,1)} %bitcast.7) | data formatting | bytes 147456

commit v5 on v4

--- a/solution.py
+++ b/solution.py
@@ -93,8 +93,6 @@
             CODE[m, t : t + 1] = row * (before + 1.0)
             before += row
 
-    pl.semaphore_wait(barrier, greeted)
-
     def ag_copy(m, p, s, o):
         axes = order[p]
         at = [me[0], me[1], me[2]]
@@ -225,27 +223,26 @@
             src_ref=X.at[m], dst_ref=OB.at[m], send_sem=pp_s.at[1, m], recv_sem=pp_r.at[1, m],
             device_id=above, device_id_type=MESH)
 
-    def take_input(m):
-        @pl.when(sec == 0)
-        def _():
-            for t in range(n_tok):
-                X[m, t : t + 1] = acts[t, m : m + 1]
-
-        @pl.when(sec == 1)
-        def _():
-            base_copy(m).wait_recv()
-            for p in range(3):
-                own_copy(m, p).wait_recv()
-                tp_copy(m, p, 0).wait_recv()
-            X[m] = (BL[m] + (TL[m].astype(F32) + TR[0, m].astype(F32))).astype(BF16)
-            back_copy(m).start()
-
-    def norm_and_send(m):
+    def own_input(m):
+        for t in range(n_tok):
+            X[m, t : t + 1] = acts[t, m : m + 1]
+
+    def passed_input(m):
+        base_copy(m).wait_recv()
+        for p in range(3):
+            own_copy(m, p).wait_recv()
+            tp_copy(m, p, 0).wait_recv()
+        X[m] = (BL[m] + (TL[m].astype(F32) + TR[0, m].astype(F32))).astype(BF16)
+        back_copy(m).start()
+
+    def norm(m):
         wide = X[m].astype(F32)
         spread = jnp.mean(wide * wide, axis=-1, keepdims=True)
         normed = (wide * lax.rsqrt(spread + 1e-06) * gain[...].astype(F32)).astype(BF16)
         G[m, me[0], me[1], me[2], :, pl.ds(0, width)] = normed
         G[m, me[0], me[1], me[2], :, pl.ds(width, LANES)] = CODE[m].astype(BF16)
+
+    def send(m):
         for p in range(3):
             ag_start(m, p, 0)
 
@@ -352,8 +349,9 @@
                 out[0, t, m : m + 1] = done[t : t + 1]
 
     def enter(m):
-        take_input(m)
-        norm_and_send(m)
+        passed_input(m)
+        norm(m)
+        send(m)
 
     def gather(m, s):
         for p in range(3):
@@ -382,14 +380,34 @@
                 def _():
                     own_copy(m, p).start()
 
+    def sent_gather(m):
+        for p in range(3):
+            for s in range(2):
+                for o in range(1, sizes[order[p][s]]):
+                    ag_copy(m, p, s, o).wait_send()
+            for k in range(5):
+                for way in range(2):
+                    far_gather(m, p, way, k).wait_send()
+
+    def sent_reduce(m):
+        for p in range(3):
+            for s in range(1, 3):
+                for o in range(1, sizes[order[p][2 - s]]):
+                    rs_copy(m, p, s, o).wait_send()
+            for k in range(5):
+                for way in range(2):
+                    far_reduce(m, p, way, k).wait_send()
+
     def only(section, *steps):
         @pl.when(sec == section)
         def _():
             for step in steps:
                 step()
 
-    enter(0)
-    only(0, lambda: enter(1))
+    only(0, lambda: own_input(0), lambda: norm(0), lambda: own_input(1), lambda: norm(1))
+    pl.semaphore_wait(barrier, greeted)
+    only(0, lambda: send(0), lambda: send(1))
+    only(1, lambda: enter(0))
     gather(0, 0)
     only(1, lambda: enter(1))
     gather(1, 0)
@@ -411,23 +429,18 @@
     reduce(0, 0)
     reduce(1, 0)
     reduce(0, 1)
+    sent_gather(0)
     reduce(1, 1)
+    sent_gather(1)
     reduce(0, 2)
     reduce(1, 2)
+    sent_reduce(0)
+    sent_reduce(1)
     finish(0)
     finish(1)
 
     for m in range(n_micro):
         for p in range(3):
-            for s in range(2):
-                for o in range(1, sizes[order[p][s]]):
-                    ag_copy(m, p, s, o).wait_send()
-                for o in range(1, sizes[order[p][1 - s]]):
-                    rs_copy(m, p, s + 1, o).wait_send()
-            for k in range(5):
-                for way in range(2):
-                    far_gather(m, p, way, k).wait_send()
-                    far_reduce(m, p, way, k).wait_send()
             tp_copy(m, p, sec).wait_send()
 
         @pl.when(sec == 0)

time: 111 us -> 111 us (level)
  no operation moved by 1% of the time
where the time goes in v5:
time: 111 us; the launch traced here: 110 us
  Pallas kernels  109 us (98%)
  local copies, waits for them, and re-layouts  1.57 us (1%)
    pallas_call x1, Pallas kernels, in_vmem(): pl.pallas_call(functools.partial(kernel, cfg), out_shape=jax.ShapeDtypeSt...  109 us

profile of v5, /device:TPU:1, one launch (start us, length us, event | category | flops | bytes accessed | tf_op | source)
XLA Modules:
  0.0 110.4 jit_solution(17715303511376637624)
XLA Ops:
  0.0 108.9 %relay.1 = bf16[1,6,2,3072]{3,2,1,0:T(2,128)(2,1)} custom-call(bf16[6,2,3072]{2,1,0:T(2,128)(2,1)} %bitcast.10, s32[1,6,2,8]{3,2,1,0:T(2,128)} %bitcast.11, bf16[1,3072]{1,0:T(2,128)(2,1)} %refs_2_.1, bf16[1,96,3072]{2,1,0:T(8,128)(2,1)} %bitcast.6, bf16[1,48,3072]{2,1,0:T(8,128)(2,1)} %bitcast.8, bf16[1,48,3072]{2,1,0:T(8,128)(2,1)} %bitcast.9, ...), custom_call_target="tpu_custom_call" | custom-call | tf_op jit(solution)/shard_map/relay/pallas_call | solution.py:519
  108.9 1.6 %copy.12 = bf16[1,2,6,3072]{3,1,2,0:T(2,128)(2,1)} copy(bf16[1,2,6,3072]{3,1,2,0:T(2,128)(2,1)} %bitcast.7) | data formatting | bytes 147456

commit v6 on v5

--- a/solution.py
+++ b/solution.py
@@ -197,8 +197,7 @@
                     at = [slice(None)] * 3
                     at[axis] = lax.rem(me[axis] + (1, sizes[axis] - 1)[way], sizes[axis])
                     where = (m, *at, slice(None), pl.ds(offs[p] + way * half + k * quarter, quarter))
-                    come = RA[m, p, way, :, :, :, pl.ds(k * quarter, quarter)].astype(F32)
-                    PT[where] = (PT[where].astype(F32) + come).astype(BF16)
+                    PT[where] = PT[where] + RA[m, p, way, :, :, :, pl.ds(k * quarter, quarter)]
                     far_reduce(m, p, way, k + 3).start()
 
     def tp_copy(m, p, section):

time: 111 us -> 110 us (level)
  no operation moved by 1% of the time
where the time goes in v6:
time: 110 us
  Pallas kernels  109 us (99%)
  local copies, waits for them, and re-layouts  1.57 us (1%)
    pallas_call x1, Pallas kernels, in_vmem(): pl.pallas_call(functools.partial(kernel, cfg), out_shape=jax.ShapeDtypeSt...  109 us

profile of v6, /device:TPU:1, one launch (start us, length us, event | category | flops | bytes accessed | tf_op | source)
XLA Modules:
  0.0 110.2 jit_solution(9670910878465109321)
XLA Ops:
  0.0 108.6 %relay.1 = bf16[1,6,2,3072]{3,2,1,0:T(2,128)(2,1)} custom-call(bf16[6,2,3072]{2,1,0:T(2,128)(2,1)} %bitcast.10, s32[1,6,2,8]{3,2,1,0:T(2,128)} %bitcast.11, bf16[1,3072]{1,0:T(2,128)(2,1)} %refs_2_.1, bf16[1,96,3072]{2,1,0:T(8,128)(2,1)} %bitcast.6, bf16[1,48,3072]{2,1,0:T(8,128)(2,1)} %bitcast.8, bf16[1,48,3072]{2,1,0:T(8,128)(2,1)} %bitcast.9, ...), custom_call_target="tpu_custom_call" | custom-call | tf_op jit(solution)/shard_map/relay/pallas_call | solution.py:518
  108.6 1.6 %copy.12 = bf16[1,2,6,3072]{3,1,2,0:T(2,128)(2,1)} copy(bf16[1,2,6,3072]{3,1,2,0:T(2,128)(2,1)} %bitcast.7) | data formatting | bytes 147456
